TPU v7x, 512 devices: a whole 4x8x8 slice. The times are simulated.
512 devices in a mesh: dp: 16 (over z_lo, y), expert: 32 (over x, z_hi, core).
Axes of the slice: x: 4, y: 8, z: 8 (z_hi: 4, z_lo: 2; z = z_hi * 2 + z_lo), core: 2. Of those that a mesh axis runs over, the one named last changes fastest.
Arguments:
- tokens: bfloat16 [32768, 2560], P(('dp', 'expert')), may hold values from -6 to 6
- expert_ids: int32 [32768, 6], P(('dp', 'expert')), may hold values from 0 to 31, all different within a row; in each aligned block of 64 rows (0 to 63, 64 to 127, ...) at most 16 rows name the same one
- gate_scores: float32 [32768, 6], P(('dp', 'expert')), may hold values from 0.02 to 0.4
- w_gate: bfloat16 [32, 2560, 768], P('expert', 'dp'), may hold values from -0.125 to 0.125
- w_up: bfloat16 [32, 2560, 768], P('expert', 'dp'), may hold values from -0.125 to 0.125
- w_down: bfloat16 [32, 768, 2560], P('expert', None, 'dp'), may hold values from -0.21875 to 0.21875
Outputs:
- mixed: bfloat16 [32768, 2560], P(('dp', 'expert'))
- expert_load: int32 [32], P('expert')
- balance_loss: float32 [], replicated
Inputs may be any that keep to these rules, and one draw needn't show every extreme that they name: `expert_ids`: each row names 6 different experts. The rows of one device name any one expert at most 16 times, and in every draw some device names some expert exactly 16 times.
All inputs are finite; a program needn't handle non-finite values.
Results may differ from a plain program's by a relative error of at most 0.0085.
Values may be sent and summed in bfloat16 or wider, within the bound.
A program may use at most 64 MiB of HBM per device.

v0:
```python
import jax
import jax.numpy as jnp
from jax import lax
from jax.sharding import Mesh
from jax.sharding import PartitionSpec as P

DP = ("dp_0", "dp_1")
DP_EXPERT = ("dp_0", "dp_1", "expert")


def sent_together(arrays, axis, dim, along):
    ends, at = ([], 0)
    for a in arrays[:-1]:
        at += a.shape[along]
        ends.append(at)
    both = jnp.concatenate(arrays, axis=along)
    return tuple(jnp.split(lax.all_gather(both, axis, axis=dim, tiled=True), ends, axis=along))


def joined_along(pieces, dim):
    lengths = list(pieces.shape[1:])
    lengths[dim] *= pieces.shape[0]
    return jnp.moveaxis(pieces, 0, dim).reshape(lengths)


def gather_in_order(value, axes, turns):
    pieces = value
    for k in turns:
        pieces = lax.all_gather(pieces, axes[k])
    done = turns[::-1]
    back = [done.index(k) for k in range(len(axes))]
    pieces = pieces.transpose(*back, *range(len(axes), pieces.ndim))
    return pieces.reshape(-1, *value.shape)


def gather_axes(value, axes, turns, dim):
    return joined_along(gather_in_order(value, axes, turns), dim)


def in_one_piece(arrays, axis, split_dim, concat_dim, along):
    widths = [a.shape[along] for a in arrays]
    both = jnp.concatenate(arrays, axis=along)
    result = lax.all_to_all(both, axis, split_axis=split_dim, concat_axis=concat_dim, tiled=True)
    return tuple(jnp.split(result, [sum(widths[:k]) for k in range(1, len(widths))], axis=along))


def copy_for_each(value, axis):
    count = lax.axis_size(axis)
    return lax.all_to_all(
        jnp.broadcast_to(value[None], (count, *value.shape)), axis, 0, 0, tiled=True
    )


def taken_together(value, axis):
    everything = copy_for_each(value, axis)
    return jnp.sum(everything, axis=0)


def packed_total(arrays, axis):
    flat, at, finished = (jnp.concatenate([a.reshape(-1) for a in arrays]), 0, [])
    running = taken_together(flat, axis)
    for a in arrays:
        finished.append(running[at : at + a.size].reshape(a.shape))
        at += a.size
    return tuple(finished)


def route_tables(expert_ids, experts, capacity):
    flat_ids = expert_ids.reshape(-1)
    onehot = (flat_ids[:, None] == jnp.arange(experts, dtype=jnp.int32)[None, :]).astype(jnp.int32)
    ranks = jnp.cumsum(onehot, axis=0) - onehot
    slot_of = jnp.sum(ranks * onehot, axis=1)
    target = flat_ids * capacity + slot_of
    return (onehot, target)


def slot_product(weights, values):
    return lax.dot_general(
        weights, values, (((0,), (0,)), ((), ())), preferred_element_type=jnp.float32
    )


def on_device(tokens, expert_ids, gate_scores, w_gate, w_up, w_down):
    tok_rows, width = tokens.shape
    topk = expert_ids.shape[1]
    experts = lax.axis_size("expert")
    groups = lax.axis_size(DP)
    capacity = 4 * tok_rows * topk // (3 * experts)
    slots = experts * capacity
    onehot, target = route_tables(expert_ids, experts, capacity)
    gate_full, up_full = sent_together((w_gate, w_up), DP, 1, 0)
    down_full = gather_axes(w_down, DP, (0, 1), 2)
    placed_flat = (jnp.arange(slots, dtype=jnp.int32)[:, None] == target[None, :]).astype(
        jnp.float32
    )
    placed = placed_flat.reshape(slots, tok_rows, topk)
    pick_send = jnp.sum(placed, axis=2).astype(jnp.bfloat16)
    outgoing = jnp.dot(pick_send, tokens, preferred_element_type=jnp.float32).astype(jnp.bfloat16)
    arrived = lax.all_to_all(
        outgoing.reshape(experts, capacity, width),
        "expert",
        split_axis=0,
        concat_axis=0,
        tiled=True,
    )
    rows = arrived.reshape(slots, width)
    gate = jnp.dot(rows, gate_full[0], preferred_element_type=jnp.float32)
    up = jnp.dot(rows, up_full[0], preferred_element_type=jnp.float32)
    hidden = (jax.nn.silu(gate) * up).astype(jnp.bfloat16)
    produced = jnp.dot(hidden, down_full[0], preferred_element_type=jnp.float32).astype(
        jnp.bfloat16
    )
    returned = lax.all_to_all(
        produced.reshape(experts, capacity, width),
        "expert",
        split_axis=0,
        concat_axis=0,
        tiled=True,
    )
    returned = returned.reshape(slots, width)
    combine = jnp.sum(placed * gate_scores[None, :, :], axis=2)
    combine_high = combine.astype(jnp.bfloat16)
    combine_low = (combine - combine_high.astype(jnp.float32)).astype(jnp.bfloat16)
    mixed = (slot_product(combine_high, returned) + slot_product(combine_low, returned)).astype(
        jnp.bfloat16
    )
    total = tok_rows * groups * experts
    flat_scores = gate_scores.reshape(-1)
    load_local = jnp.sum(onehot, axis=0).astype(jnp.float32)
    mass_local = jnp.sum(onehot.astype(jnp.float32) * flat_scores[:, None], axis=0)
    got_load, got_mass = in_one_piece((load_local[:, None], mass_local[:, None]), "expert", 0, 0, 1)
    col_load, col_mass = packed_total((jnp.sum(got_load, axis=0), jnp.sum(got_mass, axis=0)), DP)
    term = experts * col_load / (topk * total) * (col_mass / total)
    balance_loss = taken_together(jnp.sum(term), "expert")
    expert_load = col_load.astype(jnp.int32)
    return (mixed, expert_load, balance_loss)


def solution(mesh):
    split = Mesh(mesh.devices.reshape(2, 8, mesh.shape["expert"]), ("dp_0", "dp_1", "expert"))
    placed = (
        P(DP_EXPERT, None),
        P(DP_EXPERT, None),
        P(DP_EXPERT, None),
        P("expert", DP, None),
        P("expert", DP, None),
        P("expert", None, DP),
    )
    return jax.shard_map(
        on_device,
        mesh=split,
        in_specs=placed,
        out_specs=(P(DP_EXPERT, None), P("expert"), P()),
        check_vma=False,
    )
```

profile of v0, /device:TPU:64, one launch (start us, length us, event | category | flops | bytes accessed | tf_op | source)
XLA Modules:
  0.0 314.9 jit_solution(4472303451218136564)
XLA Ops:
  7.2 13.1 %all-gather = bf16[2,768,160]{1,2,0:T(8,128)(2,1)} all-gather(bf16[1,768,160]{1,2,0:T(8,128)(2,1)} %param.11), channel_id=2, replica_groups=mesh['dp_0'=2,'dp_1'=8,'expert'=32] {'dp_0'}, dimensions={0}, use_global_device_ids=true | all-gather | bytes 737280 | tf_op jit(solution)/shard_map/all_gather | solution.py:29
  20.5 1.9 pad_maximum_fusion
  23.0 0.9 reduce-window.6
  24.5 0.7 copy.64
  25.2 9.6 %all-to-all-start.2 = ((f32[32,1,2]{2,1,0:T(1,128)}), f32[32,1,2]{2,1,0:T(1,128)S(1)}, u32[]{:S(2)}, u32[]{:S(2)}) async-start(f32[32,1,2]{2,1,0:T(1,128)} %copy.64), calls=%async_computation.2 | async-start | bytes 32768 | tf_op jit(solution)/shard_map/all_to_all | solution.py:43
  35.2 9.3 %all-to-all-done.2 = f32[32,1,2]{2,1,0:T(1,128)S(1)} async-done(((f32[32,1,2]{2,1,0:T(1,128)}), f32[32,1,2]{2,1,0:T(1,128)S(1)}, u32[]{:S(2)}, u32[]{:S(2)}) %all-to-all-start.2) | async-done | bytes 288 | tf_op jit(solution)/shard_map/all_to_all | solution.py:43
  44.6 0.6 slice_reduce_fusion.2
  45.2 1.4 pad_maximum_fusion.1
  46.5 0.6 broadcast_in_dim.9
  47.2 8.6 %all-to-all-start.3 = ((f32[16,1,2]{2,1,0:T(1,128)}), f32[16,1,2]{2,1,0:T(1,128)S(1)}, u32[]{:S(2)}, u32[]{:S(2)}) async-start(f32[16,1,2]{2,1,0:T(1,128)} %broadcast_in_dim.9), calls=%async_computation.3 | async-start | bytes 16384 | tf_op jit(solution)/shard_map/all_to_all | solution.py:49
  55.8 2.3 convolution_convert_fusion.1
  58.1 4.9 %all-to-all-done.3 = f32[16,1,2]{2,1,0:T(1,128)S(1)} async-done(((f32[16,1,2]{2,1,0:T(1,128)}), f32[16,1,2]{2,1,0:T(1,128)S(1)}, u32[]{:S(2)}, u32[]{:S(2)}) %all-to-all-start.3) | async-done | bytes 160 | tf_op jit(solution)/shard_map/all_to_all | solution.py:49
  63.0 4.1 %all-to-all-start = ((bf16[32,16,2560]{2,1,0:T(8,128)(2,1)}), bf16[32,16,2560]{2,1,0:T(8,128)(2,1)S(1)}, u32[]{:S(2)}, u32[]{:S(2)}) async-start(bf16[32,16,2560]{2,1,0:T(8,128)(2,1)} %bitcast.1), calls=%async_computation | async-start | bytes 5242880 | tf_op jit(solution)/shard_map/all_to_all | solution.py:99
  68.9 8.7 %all-gather.7.cloned.1.call-done = bf16[16,768,160]{1,2,0:T(8,128)(2,1)} async-done(((bf16[2,768,160]{1,2,0:T(8,128)(2,1)}), bf16[16,768,160]{1,2,0:T(8,128)(2,1)}) %all-gather.7.cloned.1.call-update) | async-done | bytes 3932176 | tf_op jit(solution)/shard_map/all_gather | solution.py:29
  77.6 4.3 %copy.62 = bf16[2,8,1,768,160]{3,4,2,1,0:T(8,128)(2,1)} copy(bf16[2,8,1,768,160]{3,4,2,0,1:T(8,128)(2,1)} %bitcast.52) | data formatting | bytes 7864320 | tf_op jit(solution)/shard_map/transpose | solution.py:32
  81.9 128.8 %all-to-all-done = bf16[32,16,2560]{2,1,0:T(8,128)(2,1)S(1)} async-done(((bf16[32,16,2560]{2,1,0:T(8,128)(2,1)}), bf16[32,16,2560]{2,1,0:T(8,128)(2,1)S(1)}, u32[]{:S(2)}, u32[]{:S(2)}) %all-to-all-start) | async-done | bytes 2621472 | tf_op jit(solution)/shard_map/all_to_all | solution.py:99
  210.8 0.6 broadcast_in_dim.11
  211.4 3.8 %all-to-all-start.4 = ((f32[32,1,1]{2,1,0:T(1,128)}), f32[32,1,1]{2,1,0:T(1,128)S(1)}, u32[]{:S(2)}, u32[]{:S(2)}) async-start(f32[32,1,1]{2,1,0:T(1,128)} %broadcast_in_dim.11), calls=%async_computation.4 | async-start | bytes 32768 | tf_op jit(solution)/shard_map/all_to_all | solution.py:49
  215.3 5.5 %fusion.1 = f32[512,768]{1,0:T(8,128)} fusion(bf16[512,2560]{1,0:T(8,128)(2,1)S(1)} %bitcast.54, bf16[2,2560,768]{2,1,0:T(8,128)(2,1)} %all-gather.5.cloned.1.call-done), kind=kOutput, calls=%fused_computation.5 | convolution fusion | flops 2013265920 | bytes 8126464 | tf_op jit(solution)/shard_map/dot_general | solution.py:107
  220.7 10.9 %convolution_convert_fusion = bf16[512,2560]{1,0:T(8,128)(2,1)} fusion(bf16[768,2560]{0,1:T(8,128)(2,1)} %bitcast.53, f32[512,768]{1,0:T(8,128)} %fusion.1, bf16[512,2560]{1,0:T(8,128)(2,1)S(1)} %bitcast.55, bf16[2,2560,768]{2,1,0:T(8,128)(2,1)} %all-gather.5.cloned.1.call-done), kind=kOutput, calls=%fused_computation | convolution fusion | flops 4030201856 | bytes 14680064 | tf_op jit(solution)/shard_map/dot_general | solution.py:110
  231.6 9.8 %all-to-all-start.1 = ((bf16[32,16,2560]{2,1,0:T(8,128)(2,1)}), bf16[32,16,2560]{2,1,0:T(8,128)(2,1)S(1)}, u32[]{:S(2)}, u32[]{:S(2)}) async-start(bf16[32,16,2560]{2,1,0:T(8,128)(2,1)} %bitcast.56), calls=%async_computation.1 | async-start | bytes 5242880 | tf_op jit(solution)/shard_map/all_to_all | solution.py:113
  242.0 0.6 reduce_sum.102
  242.6 62.4 %all-to-all-done.1 = bf16[32,16,2560]{2,1,0:T(8,128)(2,1)S(1)} async-done(((bf16[32,16,2560]{2,1,0:T(8,128)(2,1)}), bf16[32,16,2560]{2,1,0:T(8,128)(2,1)S(1)}, u32[]{:S(2)}, u32[]{:S(2)}) %all-to-all-start.1) | async-done | bytes 2621472 | tf_op jit(solution)/shard_map/all_to_all | solution.py:113
  305.6 1.3 fusion.2
  (32 shorter events, 3.0 us)
Async XLA Ops:
  7.2 48.6 %copy-start = (bf16[64,2560]{1,0:T(8,128)(2,1)S(1)}, bf16[64,2560]{1,0:T(8,128)(2,1)}, u32[]{:S(2)}) copy-start(bf16[64,2560]{1,0:T(8,128)(2,1)} %param.6) | copy-start | bytes 983044
  7.2 15.2 %copy-start.1 = (s32[64,6]{0,1:T(8,128)S(1)}, s32[64,6]{0,1:T(8,128)}, u32[]{:S(2)}) copy-start(s32[64,6]{0,1:T(8,128)} %param.7) | copy-start | bytes 4612
  7.2 15.6 %copy-start.2 = (f32[64,6]{0,1:T(8,128)S(1)}, f32[64,6]{0,1:T(8,128)}, u32[]{:S(2)}) copy-start(f32[64,6]{0,1:T(8,128)} %param.8) | copy-start | bytes 4612
  7.2 70.4 %all-gather.7.cloned.1.call-start = ((), (), s32[]{:S(2)}) async-start(), calls=%async_computation.6 | async-start | bytes 4423680 | tf_op jit(solution)/shard_map/all_gather | solution.py:29
  20.4 194.8 %all-gather.5.cloned.1.call-start = ((), (), s32[]{:S(2)}) async-start(), calls=%async_computation.5 | async-start | bytes 8355840 | tf_op jit(solution)/shard_map/all_gather | solution.py:17
  25.2 19.3 %all-to-all-start.2 = ((f32[32,1,2]{2,1,0:T(1,128)}), f32[32,1,2]{2,1,0:T(1,128)S(1)}, u32[]{:S(2)}, u32[]{:S(2)}) async-start(f32[32,1,2]{2,1,0:T(1,128)} %copy.64), calls=%async_computation.2 | async-start | bytes 32768 | tf_op jit(solution)/shard_map/all_to_all | solution.py:43
  47.2 15.9 %all-to-all-start.3 = ((f32[16,1,2]{2,1,0:T(1,128)}), f32[16,1,2]{2,1,0:T(1,128)S(1)}, u32[]{:S(2)}, u32[]{:S(2)}) async-start(f32[16,1,2]{2,1,0:T(1,128)} %broadcast_in_dim.9), calls=%async_computation.3 | async-start | bytes 16384 | tf_op jit(solution)/shard_map/all_to_all | solution.py:49
  63.0 147.8 %all-to-all-start = ((bf16[32,16,2560]{2,1,0:T(8,128)(2,1)}), bf16[32,16,2560]{2,1,0:T(8,128)(2,1)S(1)}, u32[]{:S(2)}, u32[]{:S(2)}) async-start(bf16[32,16,2560]{2,1,0:T(8,128)(2,1)} %bitcast.1), calls=%async_computation | async-start | bytes 5242880 | tf_op jit(solution)/shard_map/all_to_all | solution.py:99
  211.4 20.2 %all-to-all-start.4 = ((f32[32,1,1]{2,1,0:T(1,128)}), f32[32,1,1]{2,1,0:T(1,128)S(1)}, u32[]{:S(2)}, u32[]{:S(2)}) async-start(f32[32,1,1]{2,1,0:T(1,128)} %broadcast_in_dim.11), calls=%async_computation.4 | async-start | bytes 32768 | tf_op jit(solution)/shard_map/all_to_all | solution.py:49
  231.6 73.4 %all-to-all-start.1 = ((bf16[32,16,2560]{2,1,0:T(8,128)(2,1)}), bf16[32,16,2560]{2,1,0:T(8,128)(2,1)S(1)}, u32[]{:S(2)}, u32[]{:S(2)}) async-start(bf16[32,16,2560]{2,1,0:T(8,128)(2,1)} %bitcast.56), calls=%async_computation.1 | async-start | bytes 5242880 | tf_op jit(solution)/shard_map/all_to_all | solution.py:113
Sparse Core Ops, SparseCore 0:
  20.5 57.0 all-gather.6
  79.7 106.1 all-gather.4
where the time goes:
time: 316 us; the launch traced here: 315 us
  waiting for transfers between devices  214 us (68%)
  starting transfers between devices  36 us (11%)
  matrix products  20.6 us (7%)
  between operations  17.1 us (5%)
  blocking collectives  13.1 us (4%)
  local copies, waits for them, and re-layouts  7.95 us (3%)
  other arithmetic  6 us (2%)
    all_to_all x1, waiting for transfers between devices, on_device(): lax.all_to_all(outgoing.reshape(experts, capacity, width), 'expert', spli...  129 us
    all_to_all x1, waiting for transfers between devices, on_device(): lax.all_to_all(produced.reshape(experts, capacity, width), 'expert', spli...  62.4 us
    all_gather x1, blocking collectives, gather_in_order(): pieces = lax.all_gather(pieces, axes[k])  13.1 us
    all_to_all x2, starting transfers between devices, copy_for_each(): lax.all_to_all(jnp.broadcast_to(value[None], (count, *value.shape)), axis...  12.4 us
    dot_general x1, matrix products, on_device(): jnp.dot(hidden, down_full[0], preferred_element_type=jnp.float32)  10.9 us
    all_to_all x1, starting transfers between devices, on_device(): lax.all_to_all(produced.reshape(experts, capacity, width), 'expert', spli...  9.79 us
    all_to_all x1, starting transfers between devices, in_one_piece(): lax.all_to_all(both, axis, split_axis=split_dim, concat_axis=concat_dim,...  9.59 us
    all_to_all x1, waiting for transfers between devices, in_one_piece(): lax.all_to_all(both, axis, split_axis=split_dim, concat_axis=concat_dim,...  9.28 us
  transfers between devices with their start and end apart: 7, of which 5 were waited for; matrix products, arithmetic and copies ran while one was open for 10% of the time, Pallas kernels for 0%

commit v1 on v0

v1 whole, which is shorter than its diff:
```python
import functools

import jax
import jax.numpy as jnp
from jax import lax
from jax.experimental import pallas as pl
from jax.experimental.pallas import tpu as pltpu
from jax.sharding import PartitionSpec as P

F32, BF16, I32 = jnp.float32, jnp.bfloat16, jnp.int32
X, ZH, C, ZL, Y = 4, 4, 2, 2, 8
CAP = 16
XC = X * C
EXPERTS = X * ZH * C
GROUPS = ZL * Y
CHUNKS = 4
RIGHT, LEFT = 1, -1


def iota(shape, dim):
    return lax.broadcasted_iota(I32, shape, dim)


def dot(a, b):
    return jnp.dot(a, b, preferred_element_type=F32)


def remote(src, dst, send, recv, dp, ex):
    return pltpu.make_async_remote_copy(
        src_ref=src,
        dst_ref=dst,
        send_sem=send,
        recv_sem=recv,
        device_id=(dp, ex),
        device_id_type=pl.DeviceIdType.MESH,
    )


def expert_of(xc, zh):
    return ((xc >> 1) * ZH + zh) * C + (xc & 1)


def expert_index(x, zh, core):
    return (x * ZH + zh) * C + core


def ring_messages(direction):
    far = "g" if direction == RIGHT else "u"
    half = 0 if direction == RIGHT else 1
    out = []
    for z in (0, 1):
        for hops in range(3):
            out += [("g", z, hops, 0, 2), ("u", z, hops, 0, 2)]
        out.append((far, z, 3, 0, 2))
    for z in (0, 1):
        out += [("d", z, 0, 0, 1), ("d", z, 0, 1, 1)]
    for z in (0, 1):
        for hops in (1, 2):
            out += [("d", z, hops, 0, 1), ("d", z, hops, 1, 1)]
        out.append(("d", z, 3, half, 1))
    return out


MESSAGES = len(ring_messages(RIGHT))
GATE_UP = 14


def kernel(
    tokens,
    ids,
    scores,
    wg,
    wu,
    wd,
    out,
    stat_out,
    gate_w,
    up_w,
    down_w,
    outgoing,
    rows,
    hidden,
    produced,
    x_in,
    partial,
    z_in,
    w_send,
    w_recv,
    w_wide,
    stat_a,
    stat_b,
    stat_mine,
    ring_send,
    ring_recv,
    zx_send,
    zx_recv,
    row_send,
    row_recv,
    w_ssem,
    w_rsem,
    sa_send,
    sa_recv,
    sb_send,
    sb_recv,
    xp_send,
    xp_recv,
    zp_send,
    zp_recv,
):
    toks, width = tokens.shape
    piece, hid = wg.shape
    half = piece // 2
    slots = EXPERTS * CAP
    span = width // CHUNKS

    dp = lax.axis_index("dp")
    me = lax.axis_index("expert")
    zl, y = dp // Y, dp % Y
    core, zh, x = me % C, (me // C) % ZH, me // (C * ZH)
    xc = x * C + core
    pos = xc * ZH + zh
    partner = (1 - zl) * Y + y

    barrier = pltpu.get_barrier_semaphore()

    def greet_expert(k, carry):
        pl.semaphore_signal(
            barrier, inc=1, device_id=(dp, (me + k) % EXPERTS), device_id_type=pl.DeviceIdType.MESH
        )
        return carry

    def greet_group(k, carry):
        pl.semaphore_signal(
            barrier, inc=1, device_id=((dp + k) % GROUPS, me), device_id_type=pl.DeviceIdType.MESH
        )
        return carry

    lax.fori_loop(1, GROUPS, greet_group, 0)
    lax.fori_loop(1, EXPERTS, greet_expert, 0)

    lanes = 128
    expert_lane = iota((toks, lanes), 1)
    named = jnp.zeros((toks, lanes), F32)
    score = jnp.zeros((toks, lanes), F32)
    for k in range(ids.shape[1]):
        hit = ids[:, k : k + 1] == expert_lane
        named = named + jnp.where(hit, 1.0, 0.0)
        score = score + jnp.where(hit, scores[:, k : k + 1], 0.0)
    earlier = (iota((toks, toks), 0) > iota((toks, toks), 1)).astype(F32).astype(BF16)
    named16 = named.astype(BF16)
    rank = dot(earlier, named16)
    rank16 = rank.astype(BF16)
    score_high = score.astype(BF16)
    score_low = (score - score_high.astype(F32)).astype(BF16)

    slot_expert = iota((lanes, slots), 1) >> 4
    spread = (iota((lanes, slots), 0) == slot_expert).astype(F32).astype(BF16)
    place = jnp.where(
        dot(rank16, spread) == (iota((toks, slots), 1) & 15).astype(F32), dot(named16, spread), 0.0
    ).astype(BF16)

    load = jnp.sum(named, axis=0, keepdims=True)
    mass = jnp.sum(score, axis=0, keepdims=True)
    row8 = iota((8, lanes), 0)
    stat_mine[0] = jnp.where(row8 == 0, load, jnp.where(row8 == 1, mass, 0.0))

    wide = 128
    slot_wide = (iota((toks, wide), 1) & 15).astype(F32)
    for z in range(ZH):
        pick = (iota((lanes, wide), 0) == expert_of(iota((lanes, wide), 1) >> 4, z)).astype(F32).astype(BF16)
        there = dot(rank16, pick) == slot_wide
        w_send[z, 0] = jnp.where(there, dot(score_high, pick), 0.0).astype(BF16)
        w_send[z, 1] = jnp.where(there, dot(score_low, pick), 0.0).astype(BF16)

    pl.semaphore_wait(barrier, EXPERTS - 1 + GROUPS - 1)

    full = {"g": gate_w, "u": up_w, "d": down_w}
    own = {"g": wg, "u": wu, "d": wd}

    def region(array, z, at, first, count):
        group = (zl if z == 0 else 1 - zl) * Y + at
        return full[array].at[pl.ds(pl.multiple_of(group * piece + first * half, 16), count * half), :]

    order = {RIGHT: ring_messages(RIGHT), LEFT: ring_messages(LEFT)}
    index = {s: {m[:4]: n for n, m in enumerate(order[s])} for s in order}
    side = {RIGHT: 0, LEFT: 1}
    arrived, started, zx_done = set(), [], set()
    zx = {}

    def start_zx(array):
        n = "gud".index(array)
        c = remote(
            own[array], region(array, 0, y, 0, 2), zx_send.at[n], zx_recv.at[n], partner, me
        )
        c.start()
        zx[array] = c

    def wait_zx(array):
        if array not in zx_done:
            zx_done.add(array)
            n = "gud".index(array)
            there = region(array, 1, y, 0, 2)
            remote(there, there, zx_send.at[n], zx_recv.at[n], partner, me).wait_recv()

    def wait_ring(s, n):
        if (s, n) in arrived:
            return
        arrived.add((s, n))
        array, z, hops, first, count = order[s][n]
        there = region(array, z, (y - s * (hops + 1) + 2 * Y) % Y, first, count)
        remote(
            there, there, ring_send.at[side[s], n], ring_recv.at[side[s], n], dp, me
        ).wait_recv()

    def forward(s, n):
        array, z, hops, first, count = order[s][n]
        at = (y - s * hops + 2 * Y) % Y
        if hops:
            if (array, z, hops - 1, first) in index[s]:
                wait_ring(s, index[s][(array, z, hops - 1, first)])
        elif z:
            wait_zx(array)
        if hops == 0 and z == 0:
            src = own[array].at[pl.ds(first * half, count * half), :]
        else:
            src = region(array, z, at, first, count)
        c = remote(
            src,
            region(array, z, at, first, count),
            ring_send.at[side[s], n],
            ring_recv.at[side[s], n],
            zl * Y + (y + s + Y) % Y,
            me,
        )
        c.start()
        started.append(c)

    def ring_step(n):
        forward(RIGHT, n)
        forward(LEFT, n)

    start_zx("g")
    start_zx("u")
    ring_step(0)
    ring_step(1)

    def send_part(k, carry):
        at = pl.ds(pl.multiple_of(k * 512, 512), 512)
        outgoing[:, at] = lax.dot_general(
            place, tokens[:, at], (((0,), (0,)), ((), ())), preferred_element_type=F32
        ).astype(BF16)
        return carry

    lax.fori_loop(0, width // 512, send_part, 0)

    def row_block(ref, n):
        return ref.at[pl.ds(pl.multiple_of(n * CAP, CAP), CAP), :]

    def row_copy(k):
        to = (me + k) % EXPERTS
        return remote(row_block(outgoing, to), row_block(rows, pos), row_send.at[k], row_recv.at[k], dp, to)

    def row_start(k, carry):
        row_copy(k).start()
        return carry

    def row_wait(k, carry):
        source = (me - k + EXPERTS) % EXPERTS
        place_of = ((source // (C * ZH)) * C + source % C) * ZH + (source // C) % ZH
        there = row_block(rows, place_of)
        remote(there, there, row_send.at[k], row_recv.at[k], dp, me).wait_recv()
        return carry

    def row_sent(k, carry):
        row_copy(k).wait_send()
        return carry

    def w_copy(k):
        to = (zh + k) % ZH
        return remote(w_send.at[to], w_recv.at[zh], w_ssem.at[k], w_rsem.at[k], dp, expert_index(x, to, core))

    def stat_a_copy(k):
        to = (dp + k) % GROUPS
        return remote(stat_mine.at[0], stat_a.at[dp], sa_send.at[k], sa_recv.at[k], to, me)

    def stat_b_copy(k):
        to = (me + k) % EXPERTS
        return remote(stat_mine.at[1], stat_b.at[me], sb_send.at[k], sb_recv.at[k], dp, to)

    def starts(copy, count):
        def one(k, carry):
            copy(k).start()
            return carry

        lax.fori_loop(1, count, one, 0)

    def sent(copy, count):
        def one(k, carry):
            copy(k).wait_send()
            return carry

        lax.fori_loop(1, count, one, 0)

    starts(stat_a_copy, GROUPS)
    for k in range(1, ZH):
        w_copy(k).start()
    lax.fori_loop(1, EXPERTS, row_start, 0)
    start_zx("d")
    stat_a[dp] = stat_mine[0]
    w_recv[zh] = w_send[zh]
    mine = pl.ds(pl.multiple_of(dp * piece, 16), piece)
    rows[pl.ds(pl.multiple_of(pos * CAP, CAP), CAP), :] = outgoing[
        pl.ds(pl.multiple_of(me * CAP, CAP), CAP), :
    ]
    gate_w[mine, :] = wg[...]
    up_w[mine, :] = wu[...]
    down_w[mine, :] = wd[...]

    ring_step(2)
    ring_step(3)

    def stat_a_wait(k, carry):
        there = stat_a.at[(dp - k + GROUPS) % GROUPS]
        remote(there, there, sa_send.at[k], sa_recv.at[k], dp, me).wait_recv()
        return carry

    lax.fori_loop(1, GROUPS, stat_a_wait, 0)
    stat_mine[1] = jnp.sum(stat_a[...], axis=0)
    starts(stat_b_copy, EXPERTS)
    stat_b[me] = stat_mine[1]

    for n in range(4, 10):
        ring_step(n)

    def stat_b_wait(k, carry):
        there = stat_b.at[(me - k + EXPERTS) % EXPERTS]
        remote(there, there, sb_send.at[k], sb_recv.at[k], dp, me).wait_recv()
        return carry

    lax.fori_loop(1, EXPERTS, stat_b_wait, 0)
    totals = jnp.sum(stat_b[...], axis=0)
    count, masses = totals[0:1, :], totals[1:2, :]
    total = toks * GROUPS * EXPERTS
    loss = jnp.sum(
        (EXPERTS * count / (ids.shape[1] * total)) * (masses / total), axis=1, keepdims=True
    )
    my_load = jnp.sum(jnp.where(iota((1, lanes), 1) == me, count, 0.0), axis=1, keepdims=True)
    stat_out[...] = jnp.where(row8 == 0, my_load, jnp.where(row8 == 1, loss, 0.0))

    for k in range(1, ZH):
        there = w_recv.at[(zh - k + ZH) % ZH]
        remote(there, there, w_ssem.at[k], w_rsem.at[k], dp, me).wait_recv()
    from_slot, to_slot = iota((wide, slots), 0), iota((wide, slots), 1)
    for z in range(ZH):
        widen = (
            ((to_slot >> 6) == (from_slot >> 4))
            & (((to_slot >> 4) & 3) == z)
            & ((to_slot & 15) == (from_slot & 15))
        )
        widen = widen.astype(F32).astype(BF16)
        for part in range(2):
            w_wide[pl.ds((part * ZH + z) * toks, toks), :] = dot(w_recv[z, part], widen).astype(BF16)

    for n in range(10, 18):
        ring_step(n)

    lax.fori_loop(1, EXPERTS, row_wait, 0)
    for s in (RIGHT, LEFT):
        for n in range(GATE_UP):
            wait_ring(s, n)

    part_width = 256
    block = slots // 2
    for n in range(hid // part_width):
        columns = slice(n * part_width, (n + 1) * part_width)

        def hidden_rows(m, carry, columns=columns):
            at = pl.ds(pl.multiple_of(m * block, block), block)
            gate = dot(rows[at, :], gate_w[:, columns])
            up = dot(rows[at, :], up_w[:, columns])
            hidden[at, columns] = (gate / (1.0 + jnp.exp(-gate)) * up).astype(BF16)
            return carry

        lax.fori_loop(0, slots // block, hidden_rows, 0)
        if n:
            ring_step(17 + n)

    def chunk_start(n):
        z = zl if n < 2 else 1 - zl
        return pl.multiple_of((z * 2 + n % 2) * span, span)

    def x_block(ref, n, at):
        return ref.at[n, pl.ds(pl.multiple_of(at * ZH * CAP, ZH * CAP), ZH * CAP), :]

    def x_copy(n):
        def copy(k):
            to = (xc + k) % XC
            return remote(
                x_block(produced, n, to),
                x_block(x_in, n, xc),
                xp_send.at[n, k],
                xp_recv.at[n, k],
                dp,
                expert_index(to // C, zh, to % C),
            )

        return copy

    def z_copy(n):
        def copy(k):
            to = (zh + k) % ZH
            return remote(
                partial.at[n, to],
                z_in.at[n, zh],
                zp_send.at[n, k],
                zp_recv.at[n, k],
                dp,
                expert_index(x, to, core),
            )

        return copy

    def produce(n):
        produced[n] = lax.dot_general(
            hidden[...],
            down_w[pl.ds(chunk_start(n), span), :],
            (((1,), (1,)), ((), ())),
            preferred_element_type=F32,
        ).astype(BF16)
        starts(x_copy(n), XC)
        at = pl.ds(pl.multiple_of(xc * ZH * CAP, ZH * CAP), ZH * CAP)
        x_in[n, at, :] = produced[n, at, :]

    def combine(n):
        def wait(k, carry):
            there = x_block(x_in, n, (xc - k + XC) % XC)
            remote(there, there, xp_send.at[n, k], xp_recv.at[n, k], dp, me).wait_recv()
            return carry

        lax.fori_loop(1, XC, wait, 0)
        both = dot(w_wide[...], x_in[n])
        summed = (both[: ZH * toks] + both[ZH * toks :]).astype(BF16)
        for z in range(ZH):
            partial[n, z] = summed[z * toks : (z + 1) * toks]
        starts(z_copy(n), ZH)
        z_in[n, zh] = partial[n, zh]

    def finish(n):
        def wait(k, carry):
            there = z_in.at[n, (zh - k + ZH) % ZH]
            remote(there, there, zp_send.at[n, k], zp_recv.at[n, k], dp, me).wait_recv()
            return carry

        lax.fori_loop(1, ZH, wait, 0)
        result = z_in[n, 0].astype(F32)
        for z in range(1, ZH):
            result = result + z_in[n, z].astype(F32)
        out[:, pl.ds(chunk_start(n), span)] = result.astype(BF16)

    def wait_down(z):
        for s in (RIGHT, LEFT):
            for n in range(GATE_UP, MESSAGES):
                if order[s][n][1] == z:
                    wait_ring(s, n)

    for n in range(20, 23):
        ring_step(n)
    wait_down(0)
    produce(0)
    ring_step(23)
    ring_step(24)
    produce(1)
    ring_step(25)
    ring_step(26)
    combine(0)
    ring_step(27)
    combine(1)
    wait_zx("d")
    wait_down(1)
    produce(2)
    produce(3)
    finish(0)
    finish(1)
    combine(2)
    combine(3)
    finish(2)
    finish(3)

    for c in started:
        c.wait_send()
    for array in "gud":
        zx[array].wait_send()
    for k in range(1, ZH):
        w_copy(k).wait_send()
    lax.fori_loop(1, EXPERTS, row_sent, 0)
    sent(stat_a_copy, GROUPS)
    sent(stat_b_copy, EXPERTS)
    for n in range(CHUNKS):
        sent(x_copy(n), XC)
        sent(z_copy(n), ZH)


def on_device(tokens, expert_ids, gate_scores, w_gate, w_up, w_down):
    toks, width = tokens.shape
    hid = w_gate.shape[2]
    slots = EXPERTS * CAP
    span = width // CHUNKS
    dma = pltpu.SemaphoreType.DMA
    vmem = pl.BlockSpec(memory_space=pltpu.VMEM)
    mixed, stats = pl.pallas_call(
        kernel,
        out_shape=(
            jax.ShapeDtypeStruct((toks, width), BF16),
            jax.ShapeDtypeStruct((8, 128), F32),
        ),
        in_specs=[vmem] * 6,
        out_specs=(vmem, vmem),
        scratch_shapes=[
            pltpu.VMEM((width, hid), BF16),
            pltpu.VMEM((width, hid), BF16),
            pltpu.VMEM((width, hid), BF16),
            pltpu.VMEM((slots, width), BF16),
            pltpu.VMEM((slots, width), BF16),
            pltpu.VMEM((slots, hid), BF16),
            pltpu.VMEM((CHUNKS, slots, span), BF16),
            pltpu.VMEM((CHUNKS, slots, span), BF16),
            pltpu.VMEM((CHUNKS, ZH, toks, span), BF16),
            pltpu.VMEM((CHUNKS, ZH, toks, span), BF16),
            pltpu.VMEM((ZH, 2, toks, 128), BF16),
            pltpu.VMEM((ZH, 2, toks, 128), BF16),
            pltpu.VMEM((2 * ZH * toks, slots), BF16),
            pltpu.VMEM((GROUPS, 8, 128), F32),
            pltpu.VMEM((EXPERTS, 8, 128), F32),
            pltpu.VMEM((2, 8, 128), F32),
            dma((2, MESSAGES)),
            dma((2, MESSAGES)),
            dma((3,)),
            dma((3,)),
            dma((EXPERTS,)),
            dma((EXPERTS,)),
            dma((ZH,)),
            dma((ZH,)),
            dma((GROUPS,)),
            dma((GROUPS,)),
            dma((EXPERTS,)),
            dma((EXPERTS,)),
            dma((CHUNKS, XC)),
            dma((CHUNKS, XC)),
            dma((CHUNKS, ZH)),
            dma((CHUNKS, ZH)),
        ],
        compiler_params=pltpu.CompilerParams(
            collective_id=0, has_side_effects=True, vmem_limit_bytes=60 * 1024 * 1024
        ),
        name="routed_layer",
    )(tokens, expert_ids, gate_scores, w_gate[0], w_up[0], w_down[0].T)
    return mixed, stats[0, :1].astype(I32), stats[1, 0]


def solution(mesh):
    both = ("dp", "expert")
    return jax.shard_map(
        on_device,
        mesh=mesh,
        in_specs=(
            P(both, None),
            P(both, None),
            P(both, None),
            P("expert", "dp", None),
            P("expert", "dp", None),
            P("expert", None, "dp"),
        ),
        out_specs=(P(both, None), P("expert"), P()),
        check_vma=False,
    )
```

time: 316 us -> 210 us (0.66)
  the two profiles are of different devices: /device:TPU:64 before, /device:TPU:1 now
where the time goes in v1:
time: 210 us; the launch traced here: 208 us
  Pallas kernels  201 us (96%)
  local copies, waits for them, and re-layouts  5.08 us (2%)
  between operations  2.43 us (1%)
    pallas_call x1, Pallas kernels, on_device(): pl.pallas_call(kernel, out_shape=(jax.ShapeDtypeStruct((toks, width), BF1...  201 us

profile of v1, /device:TPU:1, one launch (start us, length us, event | category | flops | bytes accessed | tf_op | source)
XLA Modules:
  0.0 208.4 jit_solution(10171457357534122802)
XLA Ops:
  0.6 0.0 copy-start
  0.6 1.4 copy.10.scores
  2.0 0.0 copy-done
  2.0 0.7 copy.9.ids
  2.7 200.8 %routed_layer.1 = (bf16[64,2560]{1,0:T(8,128)(2,1)}, f32[8,128]{1,0:T(8,128)}) custom-call(bf16[64,2560]{1,0:T(8,128)(2,1)} %tokens.1, s32[64,6]{1,0:T(8,128)} %copy.9.ids, f32[64,6]{1,0:T(8,128)} %copy.10.scores, bf16[160,768]{1,0:T(8,128)(2,1)} %bitcast.7, bf16[160,768]{1,0:T(8,128)(2,1)} %bitcast.8, bf16[160,768]{1,0:T(8,128)(2,1)} %bitcast.9), custom_call_target="tpu_custom_call" | custom-call | tf_op jit(solution)/shard_map/routed_layer/pallas_call | solution.py:510
  203.6 1.3 fusion
  205.5 1.7 copy.12
Async XLA Ops:
  0.6 1.4 copy-start

commit v2 on v1

v2 whole, which is shorter than its diff:
```python
import functools

import jax
import jax.numpy as jnp
from jax import lax
from jax.experimental import pallas as pl
from jax.experimental.pallas import tpu as pltpu
from jax.sharding import PartitionSpec as P

F32, BF16, I32 = jnp.float32, jnp.bfloat16, jnp.int32
X, ZH, C, ZL, Y = 4, 4, 2, 2, 8
CAP = 16
XC = X * C
EXPERTS = X * ZH * C
GROUPS = ZL * Y
RIGHT, LEFT = 1, -1
CHUNKS = (
    (0, 0, 384),
    (1, 0, 384),
    (0, 384, 256),
    (1, 384, 256),
    (0, 1024, 256),
    (0, 640, 384),
    (1, 1024, 256),
    (1, 640, 256),
    (1, 896, 128),
)


def iota(shape, dim):
    return lax.broadcasted_iota(I32, shape, dim)


def dot(a, b):
    return jnp.dot(a, b, preferred_element_type=F32)


def dot_down(a, b):
    return lax.dot_general(a, b, (((0,), (0,)), ((), ())), preferred_element_type=F32)


def dot_across(a, b):
    return lax.dot_general(a, b, (((1,), (1,)), ((), ())), preferred_element_type=F32)


def remote(src, dst, send, recv, dp, ex):
    return pltpu.make_async_remote_copy(
        src_ref=src,
        dst_ref=dst,
        send_sem=send,
        recv_sem=recv,
        device_id=(dp, ex),
        device_id_type=pl.DeviceIdType.MESH,
    )


def expert_of(xc, zh):
    return ((xc >> 1) * ZH + zh) * C + (xc & 1)


def expert_index(x, zh, core):
    return (x * ZH + zh) * C + core


def ring_messages(direction):
    far = "g" if direction == RIGHT else "u"
    half = 0 if direction == RIGHT else 1
    out = []
    for z in (0, 1):
        for hops in range(3):
            out += [("g", z, hops, 0, 2), ("u", z, hops, 0, 2)]
        out.append((far, z, 3, 0, 2))
    for hops in (0, 1):
        for z in (0, 1):
            out += [("d", z, hops, 0, 1), ("d", z, hops, 1, 1)]
    out += [("d", 0, 2, half, 1), ("d", 0, 2, 1 - half, 1)]
    out += [("d", 1, 2, half, 1), ("d", 0, 3, half, 1)]
    out += [("d", 1, 2, 1 - half, 1), ("d", 1, 3, half, 1)]
    return out


MESSAGES = len(ring_messages(RIGHT))
GATE_UP = 14


def kernel(
    tokens,
    ids,
    scores,
    wg,
    wu,
    wd,
    out,
    stat_out,
    gate_w,
    up_w,
    down_w,
    outgoing,
    rows,
    hidden,
    relative,
    w_send,
    w_recv,
    w_wide,
    stat_a,
    stat_b,
    stat_mine,
    ring_send,
    ring_recv,
    zx_send,
    zx_recv,
    row_send,
    row_recv,
    w_ssem,
    w_rsem,
    sa_send,
    sa_recv,
    sb_send,
    sb_recv,
    xp_send,
    xp_recv,
    zp_send,
    zp_recv,
    *chunk_buffers,
):
    produced, x_in, partial, z_in = (
        chunk_buffers[n * len(CHUNKS) : (n + 1) * len(CHUNKS)] for n in range(4)
    )
    toks, width = tokens.shape
    piece, hid = wg.shape
    half = piece // 2
    slots = EXPERTS * CAP
    topk = ids.shape[0]

    dp = lax.axis_index("dp")
    me = lax.axis_index("expert")
    zl, y = dp // Y, dp % Y
    core, zh, x = me % C, (me // C) % ZH, me // (C * ZH)
    xc = x * C + core
    pos = xc * ZH + zh
    partner = (1 - zl) * Y + y

    barrier = pltpu.get_barrier_semaphore()

    def greet_expert(k, carry):
        pl.semaphore_signal(
            barrier, inc=1, device_id=(dp, (me + k) % EXPERTS), device_id_type=pl.DeviceIdType.MESH
        )
        return carry

    def greet_group(k, carry):
        pl.semaphore_signal(
            barrier, inc=1, device_id=((dp + k) % GROUPS, me), device_id_type=pl.DeviceIdType.MESH
        )
        return carry

    lax.fori_loop(1, GROUPS, greet_group, 0)
    lax.fori_loop(1, EXPERTS, greet_expert, 0)

    lanes = 128
    expert_row = iota((lanes, toks), 0)
    named = jnp.zeros((lanes, toks), F32)
    score = jnp.zeros((lanes, toks), F32)
    for k in range(topk):
        hit = ids[k : k + 1, :] == expert_row
        named = named + jnp.where(hit, 1.0, 0.0)
        score = score + jnp.where(hit, scores[k : k + 1, :], 0.0)
    earlier = (iota((toks, toks), 0) < iota((toks, toks), 1)).astype(F32).astype(BF16)
    named16 = named.astype(BF16)
    rank16 = dot(named16, earlier).astype(BF16)
    score_high = score.astype(BF16)
    rest = score - score_high.astype(F32)
    score_low = rest.astype(BF16)
    score_last = (rest - score_low.astype(F32)).astype(BF16)

    ones = jnp.ones((8, toks), BF16)
    load = dot_across(ones, named16)
    mass = dot_across(ones, score_high) + dot_across(ones, score_low) + dot_across(ones, score_last)
    row8 = iota((8, lanes), 0)
    stat_mine[0] = jnp.where(row8 == 0, load, jnp.where(row8 == 1, mass, 0.0))

    spread = (iota((lanes, slots), 0) == (iota((lanes, slots), 1) >> 4)).astype(F32).astype(BF16)
    place = jnp.where(
        dot_down(rank16, spread) == (iota((toks, slots), 1) & 15).astype(F32),
        dot_down(named16, spread),
        0.0,
    ).astype(BF16)

    wide = 128
    slot_wide = (iota((toks, wide), 1) & 15).astype(F32)
    for z in range(ZH):
        pick = (iota((lanes, wide), 0) == expert_of(iota((lanes, wide), 1) >> 4, z)).astype(F32).astype(BF16)
        there = dot_down(rank16, pick) == slot_wide
        w_send[z, 0] = jnp.where(there, dot_down(score_high, pick), 0.0).astype(BF16)
        w_send[z, 1] = jnp.where(there, dot_down(score_low, pick), 0.0).astype(BF16)

    pl.semaphore_wait(barrier, EXPERTS - 1 + GROUPS - 1)

    full = {"g": gate_w, "u": up_w, "d": down_w}
    own = {"g": wg, "u": wu, "d": wd}

    def region(array, z, away, first, count):
        if array == "d":
            group = z * Y + (away + 1) % Y
            return down_w.at[pl.ds(group * piece + first * half, count * half), :]
        group = (zl if z == 0 else 1 - zl) * Y + (y + away + Y) % Y
        return full[array].at[pl.ds(pl.multiple_of(group * piece + first * half, 16), count * half), :]

    order = {RIGHT: ring_messages(RIGHT), LEFT: ring_messages(LEFT)}
    index = {s: {m[:4]: n for n, m in enumerate(order[s])} for s in order}
    side = {RIGHT: 0, LEFT: 1}
    arrived, started, zx_done = set(), [], set()
    zx = {}

    def start_zx(array):
        n = "gud".index(array)
        c = remote(
            own[array], region(array, int(array == "d"), 0, 0, 2), zx_send.at[n], zx_recv.at[n], partner, me
        )
        c.start()
        zx[array] = c

    def wait_zx(array):
        if array not in zx_done:
            zx_done.add(array)
            n = "gud".index(array)
            there = region(array, 1, 0, 0, 2)
            remote(there, there, zx_send.at[n], zx_recv.at[n], partner, me).wait_recv()

    def wait_ring(s, n):
        if (s, n) in arrived:
            return
        arrived.add((s, n))
        array, z, hops, first, count = order[s][n]
        there = region(array, z, -s * (hops + 1), first, count)
        remote(
            there, there, ring_send.at[side[s], n], ring_recv.at[side[s], n], dp, me
        ).wait_recv()

    def forward(s, n):
        array, z, hops, first, count = order[s][n]
        if hops:
            if (array, z, hops - 1, first) in index[s]:
                wait_ring(s, index[s][(array, z, hops - 1, first)])
        elif z:
            wait_zx(array)
        if hops == 0 and z == 0:
            src = own[array].at[pl.ds(first * half, count * half), :]
        else:
            src = region(array, z, -s * hops, first, count)
        if array == "d":
            dst = region(array, z, -s * (hops + 1), first, count)
        else:
            dst = region(array, z, -s * hops, first, count)
        c = remote(
            src,
            dst,
            ring_send.at[side[s], n],
            ring_recv.at[side[s], n],
            zl * Y + (y + s + Y) % Y,
            me,
        )
        c.start()
        started.append(c)

    def ring_step(n):
        forward(RIGHT, n)
        forward(LEFT, n)


    def row_block(ref, n):
        return ref.at[pl.ds(pl.multiple_of(n * CAP, CAP), CAP), :]

    def row_copy(k):
        to = (me + k) % EXPERTS
        return remote(row_block(outgoing, to), row_block(rows, pos), row_send.at[k], row_recv.at[k], dp, to)

    def row_start(k, carry):
        row_copy(k).start()
        return carry

    def row_wait(k, carry):
        source = (me - k + EXPERTS) % EXPERTS
        place_of = ((source // (C * ZH)) * C + source % C) * ZH + (source // C) % ZH
        there = row_block(rows, place_of)
        remote(there, there, row_send.at[k], row_recv.at[k], dp, me).wait_recv()
        return carry

    def row_sent(k, carry):
        row_copy(k).wait_send()
        return carry

    def w_copy(k):
        to = (zh + k) % ZH
        return remote(w_send.at[to], w_recv.at[zh], w_ssem.at[k], w_rsem.at[k], dp, expert_index(x, to, core))

    def stat_a_copy(k):
        to = (dp + k) % GROUPS
        return remote(stat_mine.at[0], stat_a.at[dp], sa_send.at[k], sa_recv.at[k], to, me)

    def stat_b_copy(k):
        to = (me + k) % EXPERTS
        return remote(stat_mine.at[1], stat_b.at[me], sb_send.at[k], sb_recv.at[k], dp, to)

    def starts(copy, count):
        def one(k, carry):
            copy(k).start()
            return carry

        lax.fori_loop(1, count, one, 0)

    def sent(copy, count):
        def one(k, carry):
            copy(k).wait_send()
            return carry

        lax.fori_loop(1, count, one, 0)

    starts(stat_a_copy, GROUPS)
    for k in range(1, ZH):
        w_copy(k).start()
    start_zx("g")
    start_zx("u")
    ring_step(0)
    ring_step(1)

    def send_part(k, carry):
        at = pl.ds(pl.multiple_of(k * 512, 512), 512)
        outgoing[:, at] = lax.dot_general(
            place, tokens[:, at], (((0,), (0,)), ((), ())), preferred_element_type=F32
        ).astype(BF16)
        return carry

    lax.fori_loop(0, width // 512, send_part, 0)

    lax.fori_loop(1, EXPERTS, row_start, 0)
    start_zx("d")
    stat_a[dp] = stat_mine[0]
    w_recv[zh] = w_send[zh]
    mine = pl.ds(pl.multiple_of(dp * piece, 16), piece)
    rows[pl.ds(pl.multiple_of(pos * CAP, CAP), CAP), :] = outgoing[
        pl.ds(pl.multiple_of(me * CAP, CAP), CAP), :
    ]
    gate_w[mine, :] = wg[...]
    up_w[mine, :] = wu[...]
    down_w[pl.ds(piece, piece), :] = wd[...]

    ring_step(2)
    ring_step(3)

    def stat_a_wait(k, carry):
        there = stat_a.at[(dp - k + GROUPS) % GROUPS]
        remote(there, there, sa_send.at[k], sa_recv.at[k], dp, me).wait_recv()
        return carry

    lax.fori_loop(1, GROUPS, stat_a_wait, 0)
    stat_mine[1] = jnp.sum(stat_a[...], axis=0)
    starts(stat_b_copy, EXPERTS)
    stat_b[me] = stat_mine[1]

    def stat_b_wait(k, carry):
        there = stat_b.at[(me - k + EXPERTS) % EXPERTS]
        remote(there, there, sb_send.at[k], sb_recv.at[k], dp, me).wait_recv()
        return carry

    for n in range(4, 8):
        ring_step(n)

    for k in range(1, ZH):
        there = w_recv.at[(zh - k + ZH) % ZH]
        remote(there, there, w_ssem.at[k], w_rsem.at[k], dp, me).wait_recv()
    from_slot, to_slot = iota((wide, slots), 0), iota((wide, slots), 1)
    for z in range(ZH):
        widen = (
            ((to_slot >> 6) == (from_slot >> 4))
            & (((to_slot >> 4) & 3) == z)
            & ((to_slot & 15) == (from_slot & 15))
        )
        widen = widen.astype(F32).astype(BF16)
        for part in range(2):
            w_wide[pl.ds((part * ZH + z) * toks, toks), :] = dot(w_recv[z, part], widen).astype(BF16)

    for n in range(8, 18):
        ring_step(n)

    lax.fori_loop(1, EXPERTS, row_wait, 0)
    for s in (RIGHT, LEFT):
        for n in range(GATE_UP):
            wait_ring(s, n)

    part_width = 256
    block = slots // 2
    for n in range(hid // part_width):
        columns = slice(n * part_width, (n + 1) * part_width)

        def hidden_rows(m, carry, columns=columns):
            at = pl.ds(pl.multiple_of(m * block, block), block)
            gate = dot(rows[at, :], gate_w[:, columns])
            up = dot(rows[at, :], up_w[:, columns])
            hidden[at, columns] = (gate / (1.0 + jnp.exp(-gate)) * up).astype(BF16)
            return carry

        lax.fori_loop(0, slots // block, hidden_rows, 0)
        if n:
            ring_step(17 + n)

    def block_of(ref, at):
        return ref.at[pl.ds(pl.multiple_of(at * ZH * CAP, ZH * CAP), ZH * CAP), :]

    def x_copy(n):
        def copy(k):
            to = (xc + k) % XC
            return remote(
                block_of(produced[n], to),
                block_of(x_in[n], xc),
                xp_send.at[n, k],
                xp_recv.at[n, k],
                dp,
                expert_index(to // C, zh, to % C),
            )

        return copy

    def z_copy(n):
        def copy(k):
            to = (zh + k) % ZH
            return remote(
                partial[n].at[to],
                z_in[n].at[zh],
                zp_send.at[n, k],
                zp_recv.at[n, k],
                dp,
                expert_index(x, to, core),
            )

        return copy

    def wait_down(z, first, columns):
        needed = range(first // piece, -(-(first + columns) // piece))
        for s in (RIGHT, LEFT):
            for m in range(GATE_UP, MESSAGES):
                if order[s][m][1] == z and (1 - s * (order[s][m][2] + 1)) % Y in needed:
                    wait_ring(s, m)

    def produce(n):
        z, first, columns = CHUNKS[n]
        wait_down(z, first, columns)
        produced[n][...] = dot_across(
            hidden[...], down_w[pl.ds(z * Y * piece + first, columns), :]
        ).astype(BF16)
        starts(x_copy(n), XC)
        at = pl.ds(pl.multiple_of(xc * ZH * CAP, ZH * CAP), ZH * CAP)
        x_in[n][at, :] = produced[n][at, :]

    def combine(n):
        def wait(k, carry):
            there = block_of(x_in[n], (xc - k + XC) % XC)
            remote(there, there, xp_send.at[n, k], xp_recv.at[n, k], dp, me).wait_recv()
            return carry

        lax.fori_loop(1, XC, wait, 0)
        both = dot(w_wide[...], x_in[n][...])
        summed = (both[: ZH * toks] + both[ZH * toks :]).astype(BF16)
        for z in range(ZH):
            partial[n][z] = summed[z * toks : (z + 1) * toks]
        starts(z_copy(n), ZH)
        z_in[n][zh] = partial[n][zh]

    def finish(n):
        def wait(k, carry):
            there = z_in[n].at[(zh - k + ZH) % ZH]
            remote(there, there, zp_send.at[n, k], zp_recv.at[n, k], dp, me).wait_recv()
            return carry

        lax.fori_loop(1, ZH, wait, 0)
        result = z_in[n][0].astype(F32)
        for z in range(1, ZH):
            result = result + z_in[n][z].astype(F32)
        z, first, columns = CHUNKS[n]
        relative[z, :, first : first + columns] = result

    def place_columns(z):
        there = pl.multiple_of((zl if z == 0 else 1 - zl) * Y * piece, Y * piece)
        turned = pltpu.roll(relative[z], ((y + Y - 1) % Y) * piece, 1)
        out[:, pl.ds(there, Y * piece)] = turned.astype(BF16)

    produce(0)
    ring_step(20)
    ring_step(21)
    produce(1)
    ring_step(22)
    ring_step(23)
    produce(2)
    combine(0)
    ring_step(24)
    produce(3)
    combine(1)
    ring_step(25)
    ring_step(26)
    produce(4)
    combine(2)
    finish(0)
    ring_step(27)
    produce(5)
    combine(3)
    finish(1)
    produce(6)
    combine(4)
    finish(2)
    produce(7)
    produce(8)

    lax.fori_loop(1, EXPERTS, stat_b_wait, 0)
    totals = jnp.sum(stat_b[...], axis=0)
    count, masses = totals[0:1, :], totals[1:2, :]
    total = toks * GROUPS * EXPERTS
    loss = jnp.sum(
        (EXPERTS * count / (topk * total)) * (masses / total), axis=1, keepdims=True
    )
    my_load = jnp.sum(jnp.where(iota((1, lanes), 1) == me, count, 0.0), axis=1, keepdims=True)
    stat_out[...] = jnp.where(row8 == 0, my_load, jnp.where(row8 == 1, loss, 0.0))

    finish(3)
    combine(5)
    finish(4)
    combine(6)
    combine(7)
    combine(8)
    finish(5)
    place_columns(0)
    finish(6)
    finish(7)
    finish(8)
    place_columns(1)

    for c in started:
        c.wait_send()
    for array in "gud":
        zx[array].wait_send()
    for k in range(1, ZH):
        w_copy(k).wait_send()
    lax.fori_loop(1, EXPERTS, row_sent, 0)
    sent(stat_a_copy, GROUPS)
    sent(stat_b_copy, EXPERTS)
    for n in range(len(CHUNKS)):
        sent(x_copy(n), XC)
        sent(z_copy(n), ZH)


def on_device(tokens, expert_ids, gate_scores, w_gate, w_up, w_down):
    toks, width = tokens.shape
    hid = w_gate.shape[2]
    slots = EXPERTS * CAP
    dma = pltpu.SemaphoreType.DMA
    vmem = pl.BlockSpec(memory_space=pltpu.VMEM)
    mixed, stats = pl.pallas_call(
        kernel,
        out_shape=(
            jax.ShapeDtypeStruct((toks, width), BF16),
            jax.ShapeDtypeStruct((8, 128), F32),
        ),
        in_specs=[vmem] * 6,
        out_specs=(vmem, vmem),
        scratch_shapes=[
            pltpu.VMEM((width, hid), BF16),
            pltpu.VMEM((width, hid), BF16),
            pltpu.VMEM((width, hid), BF16),
            pltpu.VMEM((slots, width), BF16),
            pltpu.VMEM((slots, width), BF16),
            pltpu.VMEM((slots, hid), BF16),
            pltpu.VMEM((ZL, toks, width // ZL), F32),
            pltpu.VMEM((ZH, 2, toks, 128), BF16),
            pltpu.VMEM((ZH, 2, toks, 128), BF16),
            pltpu.VMEM((2 * ZH * toks, slots), BF16),
            pltpu.VMEM((GROUPS, 8, 128), F32),
            pltpu.VMEM((EXPERTS, 8, 128), F32),
            pltpu.VMEM((2, 8, 128), F32),
            dma((2, MESSAGES)),
            dma((2, MESSAGES)),
            dma((3,)),
            dma((3,)),
            dma((EXPERTS,)),
            dma((EXPERTS,)),
            dma((ZH,)),
            dma((ZH,)),
            dma((GROUPS,)),
            dma((GROUPS,)),
            dma((EXPERTS,)),
            dma((EXPERTS,)),
            dma((len(CHUNKS), XC)),
            dma((len(CHUNKS), XC)),
            dma((len(CHUNKS), ZH)),
            dma((len(CHUNKS), ZH)),
        ]
        + [pltpu.VMEM((slots, w), BF16) for _, _, w in CHUNKS] * 2
        + [pltpu.VMEM((ZH, toks, w), BF16) for _, _, w in CHUNKS] * 2,
        compiler_params=pltpu.CompilerParams(
            collective_id=0, has_side_effects=True, vmem_limit_bytes=60 * 1024 * 1024
        ),
        name="routed_layer",
    )(tokens, expert_ids.T, gate_scores.T, w_gate[0], w_up[0], w_down[0].T)
    return mixed, stats[0, :1].astype(I32), stats[1, 0]


def solution(mesh):
    both = ("dp", "expert")
    return jax.shard_map(
        on_device,
        mesh=mesh,
        in_specs=(
            P(both, None),
            P(both, None),
            P(both, None),
            P("expert", "dp", None),
            P("expert", "dp", None),
            P("expert", None, "dp"),
        ),
        out_specs=(P(both, None), P("expert"), P()),
        check_vma=False,
    )
```

time: 210 us -> 162 us (0.77)
  Pallas kernels: 201 us -> 157 us
  local copies, waits for them, and re-layouts: 5.08 us -> 2.98 us
    pallas_call x1, Pallas kernels: 201 us -> 157 us  [on_device(): pl.pallas_call(kernel, out_shape=(jax.ShapeDtypeStruct((toks, width), BF1...]
where the time goes in v2:
time: 162 us
  Pallas kernels  157 us (97%)
  local copies, waits for them, and re-layouts  2.98 us (2%)
  between operations  2.42 us (1%)
    pallas_call x1, Pallas kernels, on_device(): pl.pallas_call(kernel, out_shape=(jax.ShapeDtypeStruct((toks, width), BF1...  157 us

profile of v2, /device:TPU:1, one launch (start us, length us, event | category | flops | bytes accessed | tf_op | source)
XLA Modules:
  0.0 162.2 jit_solution(6293453055053493012)
XLA Ops:
  0.6 156.8 %routed_layer.1 = (bf16[64,2560]{1,0:T(8,128)(2,1)}, f32[8,128]{1,0:T(8,128)}) custom-call(bf16[64,2560]{1,0:T(8,128)(2,1)} %tokens.1, s32[6,64]{1,0:T(8,128)} %bitcast.12, f32[6,64]{1,0:T(8,128)} %bitcast.13, bf16[160,768]{1,0:T(8,128)(2,1)} %bitcast.9, bf16[160,768]{1,0:T(8,128)(2,1)} %bitcast.10, bf16[160,768]{1,0:T(8,128)(2,1)} %bitcast.11), custom_call_target="tpu_custom_call" | custom-call | tf_op jit(solution)/shard_map/routed_layer/pallas_call | solution.py:556
  157.4 1.3 fusion
  159.3 1.7 %copy.10 = bf16[64,2560]{1,0:T(8,128)(2,1)} copy(bf16[64,2560]{1,0:T(8,128)(2,1)} %get-tuple-element.12) | data formatting | bytes 655360

commit v3 on v2

v3 whole, which is shorter than its diff:
```python
import functools

import jax
import jax.numpy as jnp
from jax import lax
from jax.experimental import pallas as pl
from jax.experimental.pallas import tpu as pltpu
from jax.sharding import PartitionSpec as P

F32, BF16, I32 = jnp.float32, jnp.bfloat16, jnp.int32
X, ZH, C, ZL, Y = 4, 4, 2, 2, 8
CAP = 16
XC = X * C
EXPERTS = X * ZH * C
GROUPS = ZL * Y
RIGHT, LEFT = 1, -1
CHUNKS = (
    (0, 0, 384),
    (1, 0, 384),
    (0, 384, 256),
    (0, 1024, 256),
    (0, 640, 384),
    (1, 384, 256),
    (1, 1024, 256),
    (1, 640, 256),
    (1, 896, 128),
)


def iota(shape, dim):
    return lax.broadcasted_iota(I32, shape, dim)


def dot(a, b):
    return jnp.dot(a, b, preferred_element_type=F32)


def dot_down(a, b):
    return lax.dot_general(a, b, (((0,), (0,)), ((), ())), preferred_element_type=F32)


def dot_across(a, b):
    return lax.dot_general(a, b, (((1,), (1,)), ((), ())), preferred_element_type=F32)


def remote(src, dst, send, recv, dp, ex):
    return pltpu.make_async_remote_copy(
        src_ref=src,
        dst_ref=dst,
        send_sem=send,
        recv_sem=recv,
        device_id=(dp, ex),
        device_id_type=pl.DeviceIdType.MESH,
    )


def expert_of(xc, zh):
    return ((xc >> 1) * ZH + zh) * C + (xc & 1)


def expert_index(x, zh, core):
    return (x * ZH + zh) * C + core


def ring_messages(direction):
    far = "g" if direction == RIGHT else "u"
    half = 0 if direction == RIGHT else 1
    out = []
    near = "u" if direction == RIGHT else "g"
    for hops in range(3):
        out += [("g", 0, hops, 0, 2), ("u", 0, hops, 0, 2)]
    out.append((far, 0, 3, 0, 2))
    for hops in range(2):
        out += [("g", 1, hops, 0, 2), ("u", 1, hops, 0, 2)]
    out.append((near, 1, 2, 0, 2))
    for z, hops, first in (
        [(0, 0, half), (0, 0, 1 - half), (1, 0, half), (1, 0, 1 - half), (0, 1, half), (0, 1, 1 - half)]
        + [(0, 2, half), (1, 1, half), (0, 2, 1 - half), (0, 3, half), (1, 1, 1 - half)]
        + [(1, 2, half), (1, 2, 1 - half), (1, 3, half)]
    ):
        out.append(("d", z, hops, first, 1))
    return out


MESSAGES = len(ring_messages(RIGHT))
GATE_UP = 12
SHARED = (("g", -3, RIGHT, 4), ("u", 3, LEFT, 5), ("g", -4, RIGHT, 6), ("u", 4, LEFT, 6))
PARTS = 2


def kernel(
    tokens,
    ids_in,
    scores_in,
    wg,
    wu,
    wd,
    out,
    load_out,
    loss_out,
    ids,
    scores,
    gate_w,
    up_w,
    down_w,
    hidden,
    relative,
    w_send,
    w_recv,
    w_wide,
    stat_a,
    stat_b,
    stat_mine,
    load_sem,
    ring_send,
    ring_recv,
    zx_send,
    zx_recv,
    share_send,
    share_recv,
    token_send,
    token_recv,
    row_send,
    row_recv,
    w_ssem,
    w_rsem,
    sa_send,
    sa_recv,
    sb_send,
    sb_recv,
    xp_send,
    xp_recv,
    zp_send,
    zp_recv,
    *buffers,
):
    (token_part, token_all, outgoing, rows), chunk_buffers = (
        [buffers[n * PARTS : (n + 1) * PARTS] for n in range(4)],
        buffers[4 * PARTS :],
    )
    produced, x_in, partial, z_in = (
        chunk_buffers[n * len(CHUNKS) : (n + 1) * len(CHUNKS)] for n in range(4)
    )
    toks, width = tokens.shape
    piece, hid = wg.shape
    half = piece // 2
    slots = EXPERTS * CAP
    topk = ids.shape[0]

    dp = lax.axis_index("dp")
    me = lax.axis_index("expert")
    zl, y = dp // Y, dp % Y
    core, zh, x = me % C, (me // C) % ZH, me // (C * ZH)
    xc = x * C + core
    partner = (1 - zl) * Y + y

    part = width // PARTS
    mine = pl.ds(pl.multiple_of(dp * piece, 16), piece)
    loads = [
        pltpu.make_async_copy(source, target, load_sem.at[n])
        for n, (source, target) in enumerate(
            [(ids_in, ids), (scores_in, scores)]
            + [(wg, gate_w.at[mine, :]), (wu, up_w.at[mine, :]), (wd, down_w.at[pl.ds(piece, piece), :])]
            + [(tokens.at[:, n * part : (n + 1) * part], token_part[n]) for n in range(PARTS)]
        )
    ]
    for c in loads:
        c.start()

    barrier = pltpu.get_barrier_semaphore()

    def greet_expert(k, carry):
        pl.semaphore_signal(
            barrier, inc=1, device_id=(dp, (me + k) % EXPERTS), device_id_type=pl.DeviceIdType.MESH
        )
        return carry

    def greet_group(k, carry):
        pl.semaphore_signal(
            barrier, inc=1, device_id=((dp + k) % GROUPS, me), device_id_type=pl.DeviceIdType.MESH
        )
        return carry

    lax.fori_loop(1, GROUPS, greet_group, 0)
    lax.fori_loop(1, EXPERTS, greet_expert, 0)

    for c in loads[2:5]:
        c.wait()

    pl.semaphore_wait(barrier, EXPERTS - 1 + GROUPS - 1)

    def all_of(ref, send, recv):
        return remote(ref, ref, send, recv, dp, me)

    full = {"g": gate_w, "u": up_w, "d": down_w}

    def region(array, z, away, first, count):
        if array == "d":
            group = z * Y + (away + 1) % Y
            return down_w.at[pl.ds(group * piece + first * half, count * half), :]
        group = (zl if z == 0 else 1 - zl) * Y + (y + away + Y) % Y
        return full[array].at[pl.ds(pl.multiple_of(group * piece + first * half, 16), count * half), :]

    order = {RIGHT: ring_messages(RIGHT), LEFT: ring_messages(LEFT)}
    index = {s: {m[:4]: n for n, m in enumerate(order[s])} for s in order}
    side = {RIGHT: 0, LEFT: 1}
    arrived, zx_done = set(), set()

    def start_zx(array):
        n = "gud".index(array)
        c = remote(
            region(array, 0, 0, 0, 2),
            region(array, int(array == "d"), 0, 0, 2),
            zx_send.at[0],
            zx_recv.at[n],
            partner,
            me,
        )
        c.start()

    def wait_zx(array):
        if array not in zx_done:
            zx_done.add(array)
            n = "gud".index(array)
            there = region(array, 1, 0, 0, 2)
            remote(there, there, zx_send.at[0], zx_recv.at[n], partner, me).wait_recv()

    def wait_ring(s, n):
        if (s, n) in arrived:
            return
        arrived.add((s, n))
        array, z, hops, first, count = order[s][n]
        there = region(array, z, -s * (hops + 1), first, count)
        remote(there, there, ring_send.at[side[s], 0], ring_recv.at[side[s], n], dp, me).wait_recv()

    def forward(s, n):
        array, z, hops, first, count = order[s][n]
        if hops:
            if (array, z, hops - 1, first) in index[s]:
                wait_ring(s, index[s][(array, z, hops - 1, first)])
        elif z:
            wait_zx(array)
        src = region(array, z, -s * hops, first, count)
        if array == "d":
            dst = region(array, z, -s * (hops + 1), first, count)
        else:
            dst = region(array, z, -s * hops, first, count)
        c = remote(
            src,
            dst,
            ring_send.at[side[s], int(n >= GATE_UP)],
            ring_recv.at[side[s], n],
            zl * Y + (y + s + Y) % Y,
            me,
        )
        c.start()

    def ring_step(n):
        forward(RIGHT, n)
        forward(LEFT, n)


    def block_of(ref, at):
        return ref.at[pl.ds(pl.multiple_of(at * ZH * CAP, ZH * CAP), ZH * CAP), :]

    def token_copy(n):
        def copy(k):
            to = (zh + k) % ZH
            return remote(
                token_part[n],
                block_of(token_all[n], zh),
                token_send.at[n],
                token_recv.at[n],
                dp,
                expert_index(x, to, core),
            )

        return copy

    def row_copy(n):
        def copy(k):
            to = (xc + k) % XC
            return remote(
                block_of(outgoing[n], to),
                block_of(rows[n], xc),
                row_send.at[n],
                row_recv.at[n],
                dp,
                expert_index(to // C, zh, to % C),
            )

        return copy

    def gather_send(n):
        starts(token_copy(n), ZH)
        token_all[n][pl.ds(pl.multiple_of(zh * toks, toks), toks), :] = token_part[n][...]

    def rows_send(n):
        all_of(token_all[n].at[: (ZH - 1) * toks], token_send.at[n], token_recv.at[n]).wait_recv()
        step = 256

        def some(m, carry):
            at = pl.ds(pl.multiple_of(m * step, step), step)
            outgoing[n][:, at] = dot_down(
                w_wide[2 * ZH * toks :, :], token_all[n][:, at]
            ).astype(BF16)
            return carry

        lax.fori_loop(0, part // step, some, 0)
        starts(row_copy(n), XC)
        at = pl.ds(pl.multiple_of(xc * ZH * CAP, ZH * CAP), ZH * CAP)
        rows[n][at, :] = outgoing[n][at, :]

    def rows_take(n):
        all_of(rows[n].at[: (XC - 1) * ZH * CAP], row_send.at[n], row_recv.at[n]).wait_recv()

    def share(n):
        array, away, s, m = SHARED[n]
        wait_ring(s, m)
        c = remote(
            region(array, 0, away, 0, 2),
            region(array, 0, away, 0, 2),
            share_send.at[0],
            share_recv.at[n],
            partner,
            me,
        )
        c.start()

    def wait_share(n):
        array, away, _, _ = SHARED[n]
        there = region(array, 1, away, 0, 2)
        remote(there, there, share_send.at[0], share_recv.at[n], partner, me).wait_recv()

    def w_copy(k):
        to = (zh + k) % ZH
        return remote(w_send.at[to], w_recv.at[zh], w_ssem.at[0], w_rsem.at[0], dp, expert_index(x, to, core))

    def stat_a_copy(k):
        to = (dp + k) % GROUPS
        return remote(stat_mine.at[0], stat_a.at[dp], sa_send.at[0], sa_recv.at[0], to, me)

    def stat_b_copy(k):
        to = (me + k) % EXPERTS
        return remote(stat_mine.at[1], stat_b.at[me], sb_send.at[0], sb_recv.at[0], dp, to)

    def starts(copy, count):
        def one(k, carry):
            copy(k).start()
            return carry

        lax.fori_loop(1, count, one, 0)

    ring_step(0)
    ring_step(1)

    loads[0].wait()
    loads[1].wait()

    lanes = 128
    expert_row = iota((lanes, toks), 0)
    named = jnp.zeros((lanes, toks), F32)
    score = jnp.zeros((lanes, toks), F32)
    for k in range(topk):
        hit = ids[k : k + 1, :] == expert_row
        named = named + jnp.where(hit, 1.0, 0.0)
        score = score + jnp.where(hit, scores[k : k + 1, :], 0.0)
    earlier = (iota((toks, toks), 0) < iota((toks, toks), 1)).astype(F32).astype(BF16)
    named16 = named.astype(BF16)
    rank16 = dot(named16, earlier).astype(BF16)
    score_high = score.astype(BF16)
    rest = score - score_high.astype(F32)
    score_low = rest.astype(BF16)
    score_last = (rest - score_low.astype(F32)).astype(BF16)

    ones = jnp.ones((8, toks), BF16)
    load = dot_across(ones, named16)
    mass = dot_across(ones, score_high) + dot_across(ones, score_low) + dot_across(ones, score_last)
    row8 = iota((8, lanes), 0)
    stat_mine[0] = jnp.where(row8 == 0, load, jnp.where(row8 == 1, mass, 0.0))

    wide = 128
    slot_wide = (iota((toks, wide), 1) & 15).astype(F32)
    for z in range(ZH):
        pick = (iota((lanes, wide), 0) == expert_of(iota((lanes, wide), 1) >> 4, z)).astype(F32).astype(BF16)
        there = dot_down(rank16, pick) == slot_wide
        w_send[z, 0] = jnp.where(there, dot_down(score_high, pick), 0.0).astype(BF16)
        w_send[z, 1] = jnp.where(there, dot_down(score_low, pick), 0.0).astype(BF16)
        w_send[z, 2] = jnp.where(there, dot_down(named16, pick), 0.0).astype(BF16)

    starts(stat_a_copy, GROUPS)
    for k in range(1, ZH):
        w_copy(k).start()
    loads[5].wait()
    gather_send(0)
    start_zx("g")
    loads[6].wait()
    gather_send(1)
    start_zx("u")
    start_zx("d")
    stat_a[dp] = stat_mine[0]
    w_recv[zh] = w_send[zh]

    ring_step(2)
    ring_step(3)

    all_of(w_recv.at[: ZH - 1], w_ssem.at[0], w_rsem.at[0]).wait_recv()
    from_slot, to_slot = iota((wide, slots), 0), iota((wide, slots), 1)
    for z in range(ZH):
        widen = (
            ((to_slot >> 6) == (from_slot >> 4))
            & (((to_slot >> 4) & 3) == z)
            & ((to_slot & 15) == (from_slot & 15))
        )
        widen = widen.astype(F32).astype(BF16)
        for kind in range(3):
            w_wide[pl.ds((kind * ZH + z) * toks, toks), :] = dot(w_recv[z, kind], widen).astype(BF16)

    for n in range(4, 7):
        ring_step(n)
    rows_send(0)
    ring_step(7)
    ring_step(8)
    share(0)
    share(1)
    rows_send(1)
    share(2)
    share(3)

    all_of(stat_a.at[: GROUPS - 1], sa_send.at[0], sa_recv.at[0]).wait_recv()
    stat_mine[1] = jnp.sum(stat_a[...], axis=0)
    starts(stat_b_copy, EXPERTS)
    stat_b[me] = stat_mine[1]

    for n in range(9, GATE_UP + 4):
        ring_step(n)

    rows_take(0)
    rows_take(1)
    for n in range(len(SHARED)):
        wait_share(n)
    for s in (RIGHT, LEFT):
        for n in range(GATE_UP):
            wait_ring(s, n)

    part_width = 256
    block = slots // 2
    for n in range(hid // part_width):
        columns = slice(n * part_width, (n + 1) * part_width)

        def hidden_rows(m, carry, columns=columns):
            at = pl.ds(pl.multiple_of(m * block, block), block)
            gate = sum(
                dot(rows[k][at, :], gate_w[k * part : (k + 1) * part, columns]) for k in range(PARTS)
            )
            up = sum(
                dot(rows[k][at, :], up_w[k * part : (k + 1) * part, columns]) for k in range(PARTS)
            )
            hidden[at, columns] = (gate / (1.0 + jnp.exp(-gate)) * up).astype(BF16)
            return carry

        lax.fori_loop(0, slots // block, hidden_rows, 0)
        if n:
            ring_step(GATE_UP + 3 + n)

    def x_copy(n):
        def copy(k):
            to = (xc + k) % XC
            return remote(
                block_of(produced[n], to),
                block_of(x_in[n], xc),
                xp_send.at[n],
                xp_recv.at[n],
                dp,
                expert_index(to // C, zh, to % C),
            )

        return copy

    def z_copy(n):
        def copy(k):
            to = (zh + k) % ZH
            return remote(
                partial[n].at[to],
                z_in[n].at[zh],
                zp_send.at[n],
                zp_recv.at[n],
                dp,
                expert_index(x, to, core),
            )

        return copy

    def wait_down(z, first, columns):
        needed = range(first // piece, -(-(first + columns) // piece))
        for s in (RIGHT, LEFT):
            for m in range(GATE_UP, MESSAGES):
                if order[s][m][1] == z and (1 - s * (order[s][m][2] + 1)) % Y in needed:
                    wait_ring(s, m)

    def produce(n):
        z, first, columns = CHUNKS[n]
        wait_down(z, first, columns)
        produced[n][...] = dot_across(
            hidden[...], down_w[pl.ds(z * Y * piece + first, columns), :]
        ).astype(BF16)
        starts(x_copy(n), XC)
        at = pl.ds(pl.multiple_of(xc * ZH * CAP, ZH * CAP), ZH * CAP)
        x_in[n][at, :] = produced[n][at, :]

    def combine(n):
        all_of(x_in[n].at[: (XC - 1) * ZH * CAP], xp_send.at[n], xp_recv.at[n]).wait_recv()
        both = dot(w_wide[: 2 * ZH * toks, :], x_in[n][...])
        summed = (both[: ZH * toks] + both[ZH * toks :]).astype(BF16)
        for z in range(ZH):
            partial[n][z] = summed[z * toks : (z + 1) * toks]
        starts(z_copy(n), ZH)
        z_in[n][zh] = partial[n][zh]

    def finish(n):
        all_of(z_in[n].at[: ZH - 1], zp_send.at[n], zp_recv.at[n]).wait_recv()
        result = z_in[n][0].astype(F32)
        for z in range(1, ZH):
            result = result + z_in[n][z].astype(F32)
        z, first, columns = CHUNKS[n]
        relative[z, :, first : first + columns] = result

    def place_columns(z):
        there = pl.multiple_of((zl if z == 0 else 1 - zl) * Y * piece, Y * piece)
        turned = pltpu.roll(relative[z], ((y + Y - 1) % Y) * piece, 1)
        out[:, pl.ds(there, Y * piece)] = turned.astype(BF16)

    produce(0)
    produce(1)
    ring_step(GATE_UP + 6)
    ring_step(GATE_UP + 7)
    ring_step(GATE_UP + 8)
    produce(2)
    combine(0)
    ring_step(GATE_UP + 9)
    ring_step(GATE_UP + 10)
    combine(1)
    ring_step(GATE_UP + 11)
    produce(3)
    combine(2)
    finish(0)
    produce(4)
    ring_step(GATE_UP + 12)
    produce(5)
    combine(3)
    finish(1)
    ring_step(GATE_UP + 13)
    all_of(stat_b.at[: EXPERTS - 1], sb_send.at[0], sb_recv.at[0]).wait_recv()
    totals = jnp.sum(stat_b[...], axis=0)
    count, masses = totals[0:1, :], totals[1:2, :]
    total = toks * GROUPS * EXPERTS
    loss = jnp.sum(
        (EXPERTS * count / (topk * total)) * (masses / total), axis=1, keepdims=True
    )
    my_load = jnp.sum(jnp.where(iota((1, lanes), 1) == me, count, 0.0), axis=1, keepdims=True)
    load_out[...] = my_load.astype(I32)
    loss_out[...] = loss

    finish(2)
    produce(6)
    combine(4)
    finish(3)
    produce(7)
    produce(8)
    combine(5)
    combine(6)
    finish(4)
    place_columns(0)
    combine(7)
    combine(8)
    for n in range(5, len(CHUNKS)):
        finish(n)
    place_columns(1)

    for s in (0, 1):
        all_of(gate_w.at[: GATE_UP * piece], ring_send.at[s, 0], ring_recv.at[s, 0]).wait_send()
        all_of(
            down_w.at[: (MESSAGES - GATE_UP) * half], ring_send.at[s, 1], ring_recv.at[s, 0]
        ).wait_send()
    all_of(gate_w.at[: 3 * piece], zx_send.at[0], zx_recv.at[0]).wait_send()
    all_of(gate_w.at[: len(SHARED) * piece], share_send.at[0], share_recv.at[0]).wait_send()
    all_of(w_recv.at[: ZH - 1], w_ssem.at[0], w_rsem.at[0]).wait_send()
    all_of(stat_a.at[: GROUPS - 1], sa_send.at[0], sa_recv.at[0]).wait_send()
    all_of(stat_b.at[: EXPERTS - 1], sb_send.at[0], sb_recv.at[0]).wait_send()
    for n in range(PARTS):
        all_of(token_all[n].at[: (ZH - 1) * toks], token_send.at[n], token_recv.at[n]).wait_send()
        all_of(rows[n].at[: (XC - 1) * ZH * CAP], row_send.at[n], row_recv.at[n]).wait_send()
    for n in range(len(CHUNKS)):
        all_of(x_in[n].at[: (XC - 1) * ZH * CAP], xp_send.at[n], xp_recv.at[n]).wait_send()
        all_of(z_in[n].at[: ZH - 1], zp_send.at[n], zp_recv.at[n]).wait_send()


def on_device(tokens, expert_ids, gate_scores, w_gate, w_up, w_down):
    toks, width = tokens.shape
    hid = w_gate.shape[2]
    slots = EXPERTS * CAP
    dma = pltpu.SemaphoreType.DMA
    vmem = pl.BlockSpec(memory_space=pltpu.VMEM)
    mixed, load, loss = pl.pallas_call(
        kernel,
        out_shape=(
            jax.ShapeDtypeStruct((toks, width), BF16),
            jax.ShapeDtypeStruct((1, 1), I32),
            jax.ShapeDtypeStruct((1, 1), F32),
        ),
        in_specs=[pl.BlockSpec(memory_space=pl.ANY)] * 6,
        out_specs=(vmem, vmem, vmem),
        scratch_shapes=[
            pltpu.VMEM(expert_ids.shape[::-1], I32),
            pltpu.VMEM(expert_ids.shape[::-1], F32),
            pltpu.VMEM((width, hid), BF16),
            pltpu.VMEM((width, hid), BF16),
            pltpu.VMEM((width, hid), BF16),
            pltpu.VMEM((slots, hid), BF16),
            pltpu.VMEM((ZL, toks, width // ZL), F32),
            pltpu.VMEM((ZH, 3, toks, 128), BF16),
            pltpu.VMEM((ZH, 3, toks, 128), BF16),
            pltpu.VMEM((3 * ZH * toks, slots), BF16),
            pltpu.VMEM((GROUPS, 8, 128), F32),
            pltpu.VMEM((EXPERTS, 8, 128), F32),
            pltpu.VMEM((2, 8, 128), F32),
            dma((7,)),
            dma((2, 2)),
            dma((2, MESSAGES)),
            dma((1,)),
            dma((3,)),
            dma((1,)),
            dma((len(SHARED),)),
            dma((PARTS,)),
            dma((PARTS,)),
            dma((PARTS,)),
            dma((PARTS,)),
            dma((1,)),
            dma((1,)),
            dma((1,)),
            dma((1,)),
            dma((1,)),
            dma((1,)),
            dma((len(CHUNKS),)),
            dma((len(CHUNKS),)),
            dma((len(CHUNKS),)),
            dma((len(CHUNKS),)),
        ]
        + [pltpu.VMEM((toks, width // PARTS), BF16)] * PARTS
        + [pltpu.VMEM((ZH * toks, width // PARTS), BF16)] * PARTS
        + [pltpu.VMEM((slots, width // PARTS), BF16)] * (2 * PARTS)
        + [pltpu.VMEM((slots, w), BF16) for _, _, w in CHUNKS] * 2
        + [pltpu.VMEM((ZH, toks, w), BF16) for _, _, w in CHUNKS] * 2,
        compiler_params=pltpu.CompilerParams(
            collective_id=0, has_side_effects=True, vmem_limit_bytes=60 * 1024 * 1024
        ),
        name="routed_layer",
    )(tokens, expert_ids.T, gate_scores.T, w_gate[0], w_up[0], w_down[0].T)
    return mixed, load[0], loss[0, 0]


def solution(mesh):
    both = ("dp", "expert")
    return jax.shard_map(
        on_device,
        mesh=mesh,
        in_specs=(
            P(both, None),
            P(both, None),
            P(both, None),
            P("expert", "dp", None),
            P("expert", "dp", None),
            P("expert", None, "dp"),
        ),
        out_specs=(P(both, None), P("expert"), P()),
        check_vma=False,
    )
```

time: 162 us -> 147 us (0.907)
  Pallas kernels: 157 us -> 141 us
  between operations: 2.42 us -> 4.08 us
    pallas_call x1, Pallas kernels: 157 us -> 141 us  [on_device(): pl.pallas_call(kernel, out_shape=(jax.ShapeDtypeStruct((toks, width), BF1...]
where the time goes in v3:
time: 147 us
  Pallas kernels  141 us (96%)
  between operations  4.08 us (3%)
  local copies, waits for them, and re-layouts  1.72 us (1%)
    pallas_call x1, Pallas kernels, on_device(): pl.pallas_call(kernel, out_shape=(jax.ShapeDtypeStruct((toks, width), BF1...  141 us

profile of v3, /device:TPU:1, one launch (start us, length us, event | category | flops | bytes accessed | tf_op | source)
XLA Modules:
  0.0 147.2 jit_solution(17229572798160504638)
XLA Ops:
  0.6 141.4 %routed_layer.1 = (bf16[64,2560]{1,0:T(8,128)(2,1)}, s32[1,1]{1,0:T(1,128)}, f32[1,1]{1,0:T(1,128)}) custom-call(bf16[64,2560]{1,0:T(8,128)(2,1)} %tokens.1, s32[6,64]{1,0:T(8,128)} %bitcast.12, f32[6,64]{1,0:T(8,128)} %bitcast.13, bf16[160,768]{1,0:T(8,128)(2,1)} %bitcast.9, bf16[160,768]{1,0:T(8,128)(2,1)} %bitcast.10, bf16[160,768]{1,0:T(8,128)(2,1)} %bitcast.11), custom_call_target="tpu_custom_call" | custom-call | tf_op jit(solution)/shard_map/routed_layer/pallas_call | solution.py:604
  142.0 1.7 %copy.12 = bf16[64,2560]{1,0:T(8,128)(2,1)} copy(bf16[64,2560]{1,0:T(8,128)(2,1)} %get-tuple-element.12) | data formatting | bytes 655360

commit v4 on v3

--- a/solution.py
+++ b/solution.py
@@ -68,14 +68,14 @@
     out = []
     near = "u" if direction == RIGHT else "g"
     for hops in range(3):
-        out += [("g", 0, hops, 0, 2), ("u", 0, hops, 0, 2)]
+        out += [(far, 0, hops, 0, 2), (near, 0, hops, 0, 2)]
     out.append((far, 0, 3, 0, 2))
     for hops in range(2):
-        out += [("g", 1, hops, 0, 2), ("u", 1, hops, 0, 2)]
+        out += [(near, 1, hops, 0, 2), (far, 1, hops, 0, 2)]
     out.append((near, 1, 2, 0, 2))
     for z, hops, first in (
         [(0, 0, half), (0, 0, 1 - half), (1, 0, half), (1, 0, 1 - half), (0, 1, half), (0, 1, 1 - half)]
-        + [(0, 2, half), (1, 1, half), (0, 2, 1 - half), (0, 3, half), (1, 1, 1 - half)]
+        + [(1, 1, half), (0, 2, half), (1, 1, 1 - half), (0, 2, 1 - half), (0, 3, half)]
         + [(1, 2, half), (1, 2, 1 - half), (1, 3, half)]
     ):
         out.append(("d", z, hops, first, 1))
@@ -84,7 +84,7 @@
 
 MESSAGES = len(ring_messages(RIGHT))
 GATE_UP = 12
-SHARED = (("g", -3, RIGHT, 4), ("u", 3, LEFT, 5), ("g", -4, RIGHT, 6), ("u", 4, LEFT, 6))
+SHARED = (("g", -3, RIGHT, 4), ("u", 3, LEFT, 4), ("g", -4, RIGHT, 6), ("u", 4, LEFT, 6))
 PARTS = 2
 
 
@@ -263,19 +263,31 @@
     def block_of(ref, at):
         return ref.at[pl.ds(pl.multiple_of(at * ZH * CAP, ZH * CAP), ZH * CAP), :]
 
-    def token_copy(n):
-        def copy(k):
-            to = (zh + k) % ZH
-            return remote(
-                token_part[n],
-                block_of(token_all[n], zh),
-                token_send.at[n],
-                token_recv.at[n],
-                dp,
-                expert_index(x, to, core),
-            )
-
-        return copy
+    def token_copy(n, step):
+        return remote(
+            token_part[n],
+            block_of(token_all[n], zh),
+            token_send.at[n],
+            token_recv.at[n, step % ZH],
+            dp,
+            expert_index(x, (zh + step + ZH) % ZH, core),
+        )
+
+    def relay_copy(n):
+        step = 1 if n == 0 else -1
+        at = block_of(token_all[n], (zh - step + ZH) % ZH)
+        return remote(
+            at,
+            at,
+            token_send.at[n],
+            token_recv.at[n, 2],
+            dp,
+            expert_index(x, (zh + step + ZH) % ZH, core),
+        )
+
+    def wait_tokens(n, step):
+        there = block_of(token_all[n], (zh - step + ZH) % ZH)
+        remote(there, there, token_send.at[n], token_recv.at[n, step % ZH], dp, me).wait_recv()
 
     def row_copy(n):
         def copy(k):
@@ -291,12 +303,15 @@
 
         return copy
 
-    def gather_send(n):
-        starts(token_copy(n), ZH)
+    def gather_send(n, step):
+        token_copy(n, step).start()
+
+    def gather_own(n):
         token_all[n][pl.ds(pl.multiple_of(zh * toks, toks), toks), :] = token_part[n][...]
 
     def rows_send(n):
-        all_of(token_all[n].at[: (ZH - 1) * toks], token_send.at[n], token_recv.at[n]).wait_recv()
+        wait_tokens(n, -1 if n == 0 else 1)
+        wait_tokens(n, 2)
         step = 256
 
         def some(m, carry):
@@ -310,6 +325,10 @@
         starts(row_copy(n), XC)
         at = pl.ds(pl.multiple_of(xc * ZH * CAP, ZH * CAP), ZH * CAP)
         rows[n][at, :] = outgoing[n][at, :]
+
+    def relay(n):
+        wait_tokens(n, 1 if n == 0 else -1)
+        relay_copy(n).start()
 
     def rows_take(n):
         all_of(rows[n].at[: (XC - 1) * ZH * CAP], row_send.at[n], row_recv.at[n]).wait_recv()
@@ -392,17 +411,22 @@
     for k in range(1, ZH):
         w_copy(k).start()
     loads[5].wait()
-    gather_send(0)
-    start_zx("g")
     loads[6].wait()
-    gather_send(1)
-    start_zx("u")
-    start_zx("d")
+    gather_send(0, 1)
+    gather_send(1, -1)
+    gather_send(1, 1)
+    gather_send(0, -1)
+    gather_own(0)
+    gather_own(1)
     stat_a[dp] = stat_mine[0]
     w_recv[zh] = w_send[zh]
 
     ring_step(2)
     ring_step(3)
+    relay(0)
+    relay(1)
+    for array in "gud":
+        start_zx(array)
 
     all_of(w_recv.at[: ZH - 1], w_ssem.at[0], w_rsem.at[0]).wait_recv()
     from_slot, to_slot = iota((wide, slots), 0), iota((wide, slots), 1)
@@ -416,14 +440,15 @@
         for kind in range(3):
             w_wide[pl.ds((kind * ZH + z) * toks, toks), :] = dot(w_recv[z, kind], widen).astype(BF16)
 
-    for n in range(4, 7):
-        ring_step(n)
+    ring_step(4)
+    ring_step(5)
     rows_send(0)
+    rows_send(1)
+    ring_step(6)
+    share(0)
+    share(1)
     ring_step(7)
     ring_step(8)
-    share(0)
-    share(1)
-    rows_send(1)
     share(2)
     share(3)
 
@@ -460,8 +485,7 @@
             return carry
 
         lax.fori_loop(0, slots // block, hidden_rows, 0)
-        if n:
-            ring_step(GATE_UP + 3 + n)
+        ring_step(GATE_UP + 4 + n)
 
     def x_copy(n):
         def copy(k):
@@ -532,24 +556,24 @@
 
     produce(0)
     produce(1)
-    ring_step(GATE_UP + 6)
     ring_step(GATE_UP + 7)
     ring_step(GATE_UP + 8)
-    produce(2)
     combine(0)
     ring_step(GATE_UP + 9)
+    produce(2)
+    combine(1)
     ring_step(GATE_UP + 10)
-    combine(1)
     ring_step(GATE_UP + 11)
+    combine(2)
+    produce(5)
+    ring_step(GATE_UP + 12)
+    finish(0)
     produce(3)
-    combine(2)
-    finish(0)
     produce(4)
-    ring_step(GATE_UP + 12)
-    produce(5)
-    combine(3)
     finish(1)
     ring_step(GATE_UP + 13)
+    combine(5)
+    combine(3)
     all_of(stat_b.at[: EXPERTS - 1], sb_send.at[0], sb_recv.at[0]).wait_recv()
     totals = jnp.sum(stat_b[...], axis=0)
     count, masses = totals[0:1, :], totals[1:2, :]
@@ -564,17 +588,18 @@
     finish(2)
     produce(6)
     combine(4)
-    finish(3)
     produce(7)
     produce(8)
-    combine(5)
+    finish(5)
+    finish(3)
     combine(6)
+    combine(7)
+    combine(8)
     finish(4)
     place_columns(0)
-    combine(7)
-    combine(8)
-    for n in range(5, len(CHUNKS)):
-        finish(n)
+    finish(6)
+    finish(7)
+    finish(8)
     place_columns(1)
 
     for s in (0, 1):
@@ -588,7 +613,7 @@
     all_of(stat_a.at[: GROUPS - 1], sa_send.at[0], sa_recv.at[0]).wait_send()
     all_of(stat_b.at[: EXPERTS - 1], sb_send.at[0], sb_recv.at[0]).wait_send()
     for n in range(PARTS):
-        all_of(token_all[n].at[: (ZH - 1) * toks], token_send.at[n], token_recv.at[n]).wait_send()
+        all_of(token_all[n].at[: (ZH - 1) * toks], token_send.at[n], token_recv.at[n, 0]).wait_send()
         all_of(rows[n].at[: (XC - 1) * ZH * CAP], row_send.at[n], row_recv.at[n]).wait_send()
     for n in range(len(CHUNKS)):
         all_of(x_in[n].at[: (XC - 1) * ZH * CAP], xp_send.at[n], xp_recv.at[n]).wait_send()
@@ -632,7 +657,7 @@
             dma((1,)),
             dma((len(SHARED),)),
             dma((PARTS,)),
-            dma((PARTS,)),
+            dma((PARTS, ZH)),
             dma((PARTS,)),
             dma((PARTS,)),
             dma((1,)),

time: 147 us -> 143 us (0.973)
  Pallas kernels: 141 us -> 136 us
    pallas_call x1, Pallas kernels: 141 us -> 136 us  [on_device(): pl.pallas_call(kernel, out_shape=(jax.ShapeDtypeStruct((toks, width), BF1...]
where the time goes in v4:
time: 143 us; the launch traced here: 142 us
  Pallas kernels  136 us (95%)
  between operations  4.08 us (3%)
  local copies, waits for them, and re-layouts  1.72 us (1%)
    pallas_call x1, Pallas kernels, on_device(): pl.pallas_call(kernel, out_shape=(jax.ShapeDtypeStruct((toks, width), BF1...  136 us

profile of v4, /device:TPU:1, one launch (start us, length us, event | category | flops | bytes accessed | tf_op | source)
XLA Modules:
  0.0 141.7 jit_solution(9111286424738781092)
XLA Ops:
  0.6 135.9 %routed_layer.1 = (bf16[64,2560]{1,0:T(8,128)(2,1)}, s32[1,1]{1,0:T(1,128)}, f32[1,1]{1,0:T(1,128)}) custom-call(bf16[64,2560]{1,0:T(8,128)(2,1)} %tokens.1, s32[6,64]{1,0:T(8,128)} %bitcast.12, f32[6,64]{1,0:T(8,128)} %bitcast.13, bf16[160,768]{1,0:T(8,128)(2,1)} %bitcast.9, bf16[160,768]{1,0:T(8,128)(2,1)} %bitcast.10, bf16[160,768]{1,0:T(8,128)(2,1)} %bitcast.11), custom_call_target="tpu_custom_call" | custom-call | tf_op jit(solution)/shard_map/routed_layer/pallas_call | solution.py:629
  136.6 1.7 %copy.12 = bf16[64,2560]{1,0:T(8,128)(2,1)} copy(bf16[64,2560]{1,0:T(8,128)(2,1)} %get-tuple-element.12) | data formatting | bytes 655360

commit v5 on v4

--- a/solution.py
+++ b/solution.py
@@ -15,10 +15,11 @@
 GROUPS = ZL * Y
 RIGHT, LEFT = 1, -1
 CHUNKS = (
-    (0, 0, 384),
-    (1, 0, 384),
+    (0, 0, 128),
+    (0, 128, 256),
     (0, 384, 256),
     (0, 1024, 256),
+    (1, 0, 384),
     (0, 640, 384),
     (1, 384, 256),
     (1, 1024, 256),
@@ -74,9 +75,9 @@
         out += [(near, 1, hops, 0, 2), (far, 1, hops, 0, 2)]
     out.append((near, 1, 2, 0, 2))
     for z, hops, first in (
-        [(0, 0, half), (0, 0, 1 - half), (1, 0, half), (1, 0, 1 - half), (0, 1, half), (0, 1, 1 - half)]
-        + [(1, 1, half), (0, 2, half), (1, 1, 1 - half), (0, 2, 1 - half), (0, 3, half)]
-        + [(1, 2, half), (1, 2, 1 - half), (1, 3, half)]
+        [(0, 0, half), (0, 0, 1 - half), (0, 1, half), (0, 1, 1 - half)]
+        + [(0, 2, half), (0, 2, 1 - half), (0, 3, half)]
+        + [(1, 1, half), (1, 1, 1 - half), (1, 2, half), (1, 2, 1 - half), (1, 3, half)]
     ):
         out.append(("d", z, hops, first, 1))
     return out
@@ -85,6 +86,7 @@
 MESSAGES = len(ring_messages(RIGHT))
 GATE_UP = 12
 SHARED = (("g", -3, RIGHT, 4), ("u", 3, LEFT, 4), ("g", -4, RIGHT, 6), ("u", 4, LEFT, 6))
+SHARED_DOWN = ((-1, 0), (1, 1), (-1, 1), (1, 0))
 PARTS = 2
 
 
@@ -204,7 +206,7 @@
     order = {RIGHT: ring_messages(RIGHT), LEFT: ring_messages(LEFT)}
     index = {s: {m[:4]: n for n, m in enumerate(order[s])} for s in order}
     side = {RIGHT: 0, LEFT: 1}
-    arrived, zx_done = set(), set()
+    arrived, zx_done, shared_down = set(), set(), set()
 
     def start_zx(array):
         n = "gud".index(array)
@@ -233,9 +235,30 @@
         there = region(array, z, -s * (hops + 1), first, count)
         remote(there, there, ring_send.at[side[s], 0], ring_recv.at[side[s], n], dp, me).wait_recv()
 
+    def share_down(n):
+        away, first = SHARED_DOWN[n]
+        wait_ring(-away, index[-away][("d", 0, 0, first)])
+        remote(
+            region("d", 0, away, first, 1),
+            region("d", 1, away, first, 1),
+            share_send.at[1],
+            share_recv.at[len(SHARED) + n],
+            partner,
+            me,
+        ).start()
+
+    def wait_share_down(away, first):
+        n = SHARED_DOWN.index((away, first))
+        if n not in shared_down:
+            shared_down.add(n)
+            there = region("d", 1, away, first, 1)
+            remote(there, there, share_send.at[1], share_recv.at[len(SHARED) + n], partner, me).wait_recv()
+
     def forward(s, n):
         array, z, hops, first, count = order[s][n]
-        if hops:
+        if array == "d" and z == 1 and hops == 1:
+            wait_share_down(-s, first)
+        elif hops:
             if (array, z, hops - 1, first) in index[s]:
                 wait_ring(s, index[s][(array, z, hops - 1, first)])
         elif z:
@@ -373,6 +396,15 @@
     ring_step(0)
     ring_step(1)
 
+    loads[5].wait()
+    loads[6].wait()
+    gather_send(0, 1)
+    gather_send(1, -1)
+    gather_send(1, 1)
+    gather_send(0, -1)
+    gather_own(0)
+    gather_own(1)
+
     loads[0].wait()
     loads[1].wait()
 
@@ -410,14 +442,6 @@
     starts(stat_a_copy, GROUPS)
     for k in range(1, ZH):
         w_copy(k).start()
-    loads[5].wait()
-    loads[6].wait()
-    gather_send(0, 1)
-    gather_send(1, -1)
-    gather_send(1, 1)
-    gather_send(0, -1)
-    gather_own(0)
-    gather_own(1)
     stat_a[dp] = stat_mine[0]
     w_recv[zh] = w_send[zh]
 
@@ -427,6 +451,9 @@
     relay(1)
     for array in "gud":
         start_zx(array)
+
+    ring_step(4)
+    ring_step(5)
 
     all_of(w_recv.at[: ZH - 1], w_ssem.at[0], w_rsem.at[0]).wait_recv()
     from_slot, to_slot = iota((wide, slots), 0), iota((wide, slots), 1)
@@ -440,8 +467,6 @@
         for kind in range(3):
             w_wide[pl.ds((kind * ZH + z) * toks, toks), :] = dot(w_recv[z, kind], widen).astype(BF16)
 
-    ring_step(4)
-    ring_step(5)
     rows_send(0)
     rows_send(1)
     ring_step(6)
@@ -457,7 +482,7 @@
     starts(stat_b_copy, EXPERTS)
     stat_b[me] = stat_mine[1]
 
-    for n in range(9, GATE_UP + 4):
+    for n in range(9, GATE_UP + 2):
         ring_step(n)
 
     rows_take(0)
@@ -470,22 +495,21 @@
 
     part_width = 256
     block = slots // 2
-    for n in range(hid // part_width):
-        columns = slice(n * part_width, (n + 1) * part_width)
-
-        def hidden_rows(m, carry, columns=columns):
-            at = pl.ds(pl.multiple_of(m * block, block), block)
-            gate = sum(
-                dot(rows[k][at, :], gate_w[k * part : (k + 1) * part, columns]) for k in range(PARTS)
-            )
-            up = sum(
-                dot(rows[k][at, :], up_w[k * part : (k + 1) * part, columns]) for k in range(PARTS)
-            )
-            hidden[at, columns] = (gate / (1.0 + jnp.exp(-gate)) * up).astype(BF16)
-            return carry
-
-        lax.fori_loop(0, slots // block, hidden_rows, 0)
-        ring_step(GATE_UP + 4 + n)
+    def hidden_part(n, m):
+        columns, at = slice(n * part_width, (n + 1) * part_width), slice(m * block, (m + 1) * block)
+        gate = sum(
+            dot(rows[k][at, :], gate_w[k * part : (k + 1) * part, columns]) for k in range(PARTS)
+        )
+        up = sum(dot(rows[k][at, :], up_w[k * part : (k + 1) * part, columns]) for k in range(PARTS))
+        hidden[at, columns] = (gate / (1.0 + jnp.exp(-gate)) * up).astype(BF16)
+
+    pieces = [(n, m) for n in range(hid // part_width) for m in range(slots // block)]
+    for turn in range(2):
+        for n, m in pieces[turn * len(pieces) // 2 : (turn + 1) * len(pieces) // 2]:
+            hidden_part(n, m)
+        ring_step(GATE_UP + 2 + turn)
+        share_down(2 * turn)
+        share_down(2 * turn + 1)
 
     def x_copy(n):
         def copy(k):
@@ -517,6 +541,11 @@
 
     def wait_down(z, first, columns):
         needed = range(first // piece, -(-(first + columns) // piece))
+        if z == 1 and 1 in needed:
+            wait_zx("d")
+        for away, part_of in SHARED_DOWN:
+            if z == 1 and (away + 1) % Y in needed:
+                wait_share_down(away, part_of)
         for s in (RIGHT, LEFT):
             for m in range(GATE_UP, MESSAGES):
                 if order[s][m][1] == z and (1 - s * (order[s][m][2] + 1)) % Y in needed:
@@ -556,24 +585,31 @@
 
     produce(0)
     produce(1)
+    ring_step(GATE_UP + 4)
+    combine(0)
+    ring_step(GATE_UP + 5)
+    produce(2)
+    ring_step(GATE_UP + 6)
+    combine(1)
     ring_step(GATE_UP + 7)
     ring_step(GATE_UP + 8)
-    combine(0)
-    ring_step(GATE_UP + 9)
-    produce(2)
-    combine(1)
-    ring_step(GATE_UP + 10)
-    ring_step(GATE_UP + 11)
+    produce(3)
+    produce(4)
     combine(2)
     produce(5)
-    ring_step(GATE_UP + 12)
+    ring_step(GATE_UP + 9)
+    combine(3)
+    ring_step(GATE_UP + 10)
+    produce(6)
     finish(0)
-    produce(3)
-    produce(4)
     finish(1)
-    ring_step(GATE_UP + 13)
+    ring_step(GATE_UP + 11)
+    combine(4)
+    finish(2)
+    produce(7)
     combine(5)
-    combine(3)
+    produce(8)
+    produce(9)
     all_of(stat_b.at[: EXPERTS - 1], sb_send.at[0], sb_recv.at[0]).wait_recv()
     totals = jnp.sum(stat_b[...], axis=0)
     count, masses = totals[0:1, :], totals[1:2, :]
@@ -585,21 +621,16 @@
     load_out[...] = my_load.astype(I32)
     loss_out[...] = loss
 
-    finish(2)
-    produce(6)
-    combine(4)
-    produce(7)
-    produce(8)
-    finish(5)
-    finish(3)
     combine(6)
     combine(7)
     combine(8)
+    combine(9)
+    finish(3)
     finish(4)
+    finish(5)
     place_columns(0)
-    finish(6)
-    finish(7)
-    finish(8)
+    for n in range(6, len(CHUNKS)):
+        finish(n)
     place_columns(1)
 
     for s in (0, 1):
@@ -609,6 +640,7 @@
         ).wait_send()
     all_of(gate_w.at[: 3 * piece], zx_send.at[0], zx_recv.at[0]).wait_send()
     all_of(gate_w.at[: len(SHARED) * piece], share_send.at[0], share_recv.at[0]).wait_send()
+    all_of(down_w.at[: len(SHARED_DOWN) * half], share_send.at[1], share_recv.at[0]).wait_send()
     all_of(w_recv.at[: ZH - 1], w_ssem.at[0], w_rsem.at[0]).wait_send()
     all_of(stat_a.at[: GROUPS - 1], sa_send.at[0], sa_recv.at[0]).wait_send()
     all_of(stat_b.at[: EXPERTS - 1], sb_send.at[0], sb_recv.at[0]).wait_send()
@@ -654,8 +686,8 @@
             dma((2, MESSAGES)),
             dma((1,)),
             dma((3,)),
-            dma((1,)),
-            dma((len(SHARED),)),
+            dma((2,)),
+            dma((len(SHARED) + len(SHARED_DOWN),)),
             dma((PARTS,)),
             dma((PARTS, ZH)),
             dma((PARTS,)),

time: 143 us -> 141 us (0.986)
  no operation moved by 1% of the time
where the time goes in v5:
time: 141 us
  Pallas kernels  135 us (96%)
  between operations  4.08 us (3%)
  local copies, waits for them, and re-layouts  1.72 us (1%)
    pallas_call x1, Pallas kernels, on_device(): pl.pallas_call(kernel, out_shape=(jax.ShapeDtypeStruct((toks, width), BF1...  135 us

profile of v5, /device:TPU:1, one launch (start us, length us, event | category | flops | bytes accessed | tf_op | source)
XLA Modules:
  0.0 140.7 jit_solution(7849140682739018470)
XLA Ops:
  0.6 134.9 %routed_layer.1 = (bf16[64,2560]{1,0:T(8,128)(2,1)}, s32[1,1]{1,0:T(1,128)}, f32[1,1]{1,0:T(1,128)}) custom-call(bf16[64,2560]{1,0:T(8,128)(2,1)} %tokens.1, s32[6,64]{1,0:T(8,128)} %bitcast.12, f32[6,64]{1,0:T(8,128)} %bitcast.13, bf16[160,768]{1,0:T(8,128)(2,1)} %bitcast.9, bf16[160,768]{1,0:T(8,128)(2,1)} %bitcast.10, bf16[160,768]{1,0:T(8,128)(2,1)} %bitcast.11), custom_call_target="tpu_custom_call" | custom-call | tf_op jit(solution)/shard_map/routed_layer/pallas_call | solution.py:661
  135.5 1.7 %copy.12 = bf16[64,2560]{1,0:T(8,128)(2,1)} copy(bf16[64,2560]{1,0:T(8,128)(2,1)} %get-tuple-element.12) | data formatting | bytes 655360

commit v6 on v5

--- a/solution.py
+++ b/solution.py
@@ -593,21 +593,22 @@
     combine(1)
     ring_step(GATE_UP + 7)
     ring_step(GATE_UP + 8)
+    produce(4)
     produce(3)
-    produce(4)
     combine(2)
     produce(5)
     ring_step(GATE_UP + 9)
+    combine(4)
+    ring_step(GATE_UP + 10)
     combine(3)
-    ring_step(GATE_UP + 10)
     produce(6)
+    ring_step(GATE_UP + 11)
     finish(0)
     finish(1)
-    ring_step(GATE_UP + 11)
-    combine(4)
+    combine(5)
+    produce(7)
     finish(2)
-    produce(7)
-    combine(5)
+    combine(6)
     produce(8)
     produce(9)
     all_of(stat_b.at[: EXPERTS - 1], sb_send.at[0], sb_recv.at[0]).wait_recv()
@@ -621,7 +622,6 @@
     load_out[...] = my_load.astype(I32)
     loss_out[...] = loss
 
-    combine(6)
     combine(7)
     combine(8)
     combine(9)

time: 141 us -> 140 us (level)
  no operation moved by 1% of the time
where the time goes in v6:
time: 140 us; the launch traced here: 139 us
  Pallas kernels  134 us (96%)
  between operations  4.08 us (3%)
  local copies, waits for them, and re-layouts  1.72 us (1%)
    pallas_call x1, Pallas kernels, on_device(): pl.pallas_call(kernel, out_shape=(jax.ShapeDtypeStruct((toks, width), BF1...  134 us

profile of v6, /device:TPU:1, one launch (start us, length us, event | category | flops | bytes accessed | tf_op | source)
XLA Modules:
  0.0 139.4 jit_solution(17960329052566024112)
XLA Ops:
  0.6 133.6 %routed_layer.1 = (bf16[64,2560]{1,0:T(8,128)(2,1)}, s32[1,1]{1,0:T(1,128)}, f32[1,1]{1,0:T(1,128)}) custom-call(bf16[64,2560]{1,0:T(8,128)(2,1)} %tokens.1, s32[6,64]{1,0:T(8,128)} %bitcast.12, f32[6,64]{1,0:T(8,128)} %bitcast.13, bf16[160,768]{1,0:T(8,128)(2,1)} %bitcast.9, bf16[160,768]{1,0:T(8,128)(2,1)} %bitcast.10, bf16[160,768]{1,0:T(8,128)(2,1)} %bitcast.11), custom_call_target="tpu_custom_call" | custom-call | tf_op jit(solution)/shard_map/routed_layer/pallas_call | solution.py:661
  134.2 1.7 %copy.12 = bf16[64,2560]{1,0:T(8,128)(2,1)} copy(bf16[64,2560]{1,0:T(8,128)(2,1)} %get-tuple-element.12) | data formatting | bytes 655360
